TPU v7x, 32 devices: a whole 2x2x4 slice. The times are simulated.
32 devices in a mesh: gz: 32 (over z, y, x, core).
Axes of the slice: x: 2, y: 2, z: 4, core: 2. Of those that a mesh axis runs over, the one named last changes fastest.
Arguments:
- u_face: float32 [64, 1024, 512], P('gz')
- v_face: float32 [64, 1024, 512], P('gz')
- w_face: float32 [64, 1024, 512], P('gz')
- smoke: float32 [64, 1024, 512], P('gz'), may hold values from 0 to 2
- obstacles: int32 [64, 32, 512], P('gz'), may hold values from -2147483648 to 2147483647, as said below
Outputs:
- impulse: float32 [64, 1024, 512], P('gz')
- relative_residual: float32 [64, 1024, 512], P('gz')
Inputs may be any that keep to these rules, and one draw needn't show every extreme that they name: Bit k of obstacles[z, b, x] is 1 where cell (z, 32 b + k, x) is solid and 0 where it holds fluid; every bit of a word is used.
All inputs are finite; a program needn't handle non-finite values. Where the computation divides by a largest or mean magnitude, that divisor is 1e-20 or more.
Results may differ from a plain program's by a relative error of at most 0.00011.
Values sent between devices are 32-bit elements; how exact they have to be, the bound alone decides.
A program may use at most 192 MiB of HBM per device.

v0:
```python
import functools

import jax
import jax.numpy as jnp
from jax import lax
from jax.experimental import pallas as pl
from jax.experimental.pallas import tpu as pltpu
from jax.sharding import PartitionSpec as P

EPS = 1e-06
CFL = 0.5
BUOYANCY = 100.0

ROWS = 32
PAD = 8


def kernel(n, chunks, u_hbm, v_hbm, w_hbm, s_hbm, ob_hbm, imp_hbm, res_hbm,
           u, v, w, s, z, y, code, ay, lw, lw_next, ob, cw, acc, cf, mx, mx_all, st, st_all,
           in_sem, ob_send, ob_recv, lw_send, lw_recv, dn_send, dn_recv, up_send, up_recv,
           mx_send, mx_recv, st_send, st_recv, out_sem):
    depth, ny, nx = w.shape
    nb = ny // ROWS
    crow = ny // chunks
    me = lax.axis_index("gz")
    has_low, has_high = me > 0, me < n - 1
    low, high = jnp.maximum(me - 1, 0), jnp.minimum(me + 1, n - 1)

    def at(device):
        return dict(device_id=(device,), device_id_type=pl.DeviceIdType.MESH)

    ins = [(u_hbm, u), (v_hbm, v), (w_hbm, w), (s_hbm, s)]

    def load(k, p):
        src, dst = ins[k]
        return pltpu.make_async_copy(src.at[p], dst.at[p, pl.ds(0, ny)], in_sem.at[k * depth + p])

    ob_in = pltpu.make_async_copy(ob_hbm, ob.at[pl.ds(2, depth)], in_sem.at[4 * depth])
    ob_in.start()
    for k in range(4):
        for p in range(depth):
            load(k, p).start()

    barrier = pltpu.get_barrier_semaphore()

    def greet(i, carry):
        pl.semaphore_signal(barrier, inc=1, **at(lax.rem(me + i, n)))
        return carry

    lax.fori_loop(1, n, greet, 0)

    zrow = jnp.zeros((PAD, nx), jnp.float32)
    for p in range(depth + 4):
        z[p, 0:PAD, :] = zrow
        z[p, ny + PAD : ny + 2 * PAD, :] = zrow
    for p in range(depth + 2):
        y[p, 0:PAD, :] = zrow
        y[p, ny + PAD : ny + 2 * PAD, :] = zrow
    for p in range(depth):
        v[p, ny : ny + PAD, :] = zrow
    acc[...] = jnp.zeros_like(acc)

    def zero_planes(ref, planes, offset):
        def body(i, carry):
            for p in planes:
                ref[p, pl.ds(pl.multiple_of(i * ROWS + offset, 8), ROWS), :] = jnp.zeros((ROWS, nx), jnp.float32)
            return carry
        lax.fori_loop(0, nb, body, 0)

    ob_in.wait()
    pl.semaphore_wait(barrier, n - 1)

    ob_down = pltpu.make_async_remote_copy(
        ob.at[pl.ds(2, 2)], ob.at[pl.ds(depth + 2, 2)], ob_send.at[0], ob_recv.at[0], **at(low))
    ob_up = pltpu.make_async_remote_copy(
        ob.at[pl.ds(depth, 2)], ob.at[pl.ds(0, 2)], ob_send.at[1], ob_recv.at[1], **at(high))

    @pl.when(has_low)
    def _():
        ob_down.start()

    @pl.when(has_high)
    def _():
        ob_up.start()

    @pl.when(jnp.logical_not(has_low))
    def _():
        ob[0:2] = jnp.zeros((2,) + ob.shape[1:], jnp.int32)
        zero_planes(z, (0, 1), PAD)

    @pl.when(jnp.logical_not(has_high))
    def _():
        ob[depth + 2 : depth + 4] = jnp.zeros((2,) + ob.shape[1:], jnp.int32)
        zero_planes(z, (depth + 2, depth + 3), PAD)
        zero_planes(lw_next, (0,), 0)

    mx[...] = jnp.zeros_like(mx)
    for k in range(3):
        ref = ins[k][1]
        for p in range(depth):
            load(k, p).wait()

            def body(i, m, ref=ref, p=p):
                a = jnp.abs(ref[p, pl.ds(pl.multiple_of(i * ROWS, 8), ROWS), :])
                return jnp.maximum(m, jnp.max(a.reshape(ROWS // 8, 8, nx), axis=0))

            m = lax.fori_loop(0, nb, body, jnp.zeros((8, nx), jnp.float32))
            m = jnp.max(m, axis=0, keepdims=True)
            for c in range(0, nx, 128):
                mx[...] = jnp.maximum(mx[...], jnp.broadcast_to(m[:, c : c + 128], mx.shape))

    def spread(src, dst, send, recv):
        def copy(i):
            return pltpu.make_async_remote_copy(
                src, dst.at[i], send.at[i], recv.at[i], **at(lax.rem(me + i, n)))

        def start(i, carry):
            copy(i).start()
            return carry

        def wait(i, carry):
            copy(i).wait_recv()
            copy(i).wait_send()
            return carry

        return (lambda: lax.fori_loop(1, n, start, 0)), (lambda: lax.fori_loop(1, n, wait, 0))

    mx_start, mx_wait = spread(mx, mx_all, mx_send, mx_recv)
    mx_start()

    @pl.when(has_low)
    def _():
        ob_down.wait_send()
        ob_up.wait_recv()

    @pl.when(has_high)
    def _():
        ob_up.wait_send()
        ob_down.wait_recv()

    row_id = lax.broadcasted_iota(jnp.int32, (nb, nx), 0)
    col_id = lax.broadcasted_iota(jnp.int32, (nb, nx), 1)
    srl = lax.shift_right_logical
    c1, c31 = jnp.int32(1), jnp.int32(31)
    full1, full31 = jnp.full((nb, nx), c1), jnp.full((nb, nx), c31)
    for p in range(depth + 2):
        mid = ob[p + 1]
        after = jnp.where(row_id == nb - 1, 0, pltpu.roll(mid, nb - 1, 0))
        before = jnp.where(row_id == 0, 0, pltpu.roll(mid, 1, 0))
        a = srl(mid, full1) | (after << full31)
        b = (mid << full1) | srl(before, full31)
        c = jnp.where(col_id == nx - 1, 0, pltpu.roll(mid, nx - 1, 1))
        d = jnp.where(col_id == 0, 0, pltpu.roll(mid, 1, 1))
        e, f = ob[p], ob[p + 2]
        s1, k1 = a ^ b ^ c, (a & b) | (c & (a | b))
        s2, k2 = d ^ e ^ f, (d & e) | (f & (d | e))
        k3 = s1 & s2
        cw[p, 0] = s1 ^ s2
        cw[p, 1] = k1 ^ k2 ^ k3
        cw[p, 2] = (k1 & k2) | (k3 & (k1 | k2))
        outside = None
        if p == 0:
            outside = jnp.logical_not(has_low)
        if p == depth + 1:
            outside = jnp.logical_not(has_high)
        cw[p, 3] = mid
        if outside is not None:
            @pl.when(outside)
            def _(p=p):
                cw[p, 3] = jnp.full((nb, nx), -1, jnp.int32)

    half = 16
    places = lax.broadcasted_iota(jnp.int32, (half, nx), 0)

    def code_rows(b, carry):
        for p in range(depth + 2):
            for k0 in range(0, ROWS, half):
                bits = [
                    srl(jnp.broadcast_to(cw[p, j, pl.ds(b, 1), :], (half, nx)), places + k0) & 1
                    for j in range(4)
                ]
                count = bits[0] + (bits[1] << 1) + (bits[2] << 2)
                code[p, pl.ds(pl.multiple_of(b * ROWS + k0, 8), half), :] = jnp.where(
                    bits[3] == 1, -1, 6 - count).astype(jnp.float32)
        return carry

    for p in range(depth):
        load(3, p).wait()
    mx_wait()
    mx_all[0] = mx[...]
    top = jnp.max(jnp.max(mx_all[...], axis=0), axis=1, keepdims=True)[0:1]
    top = jnp.broadcast_to(top, (1, nx))
    cf[0:1, :] = (CFL / (top + EPS)) * BUOYANCY

    lane = lax.broadcasted_iota(jnp.int32, (ROWS, nx), 1)

    def lifted(p, r):
        rows = pl.ds(r, ROWS)
        return w[p, rows, :] + cf[0:1, :] * s[p, rows, :]

    def chunked(prepare, compute, sends):
        def body(c, carry):
            @pl.when(c < chunks)
            def _():
                prepare(c)

                def inner(i, k):
                    compute(pl.multiple_of(c * crow + i * ROWS, 8))
                    return k
                lax.fori_loop(0, crow // ROWS, inner, 0)

            @pl.when(c > 0)
            def _():
                for cond, copy in sends:
                    @pl.when(cond)
                    def _(copy=copy):
                        copy(c - 1)
            return carry
        lax.fori_loop(0, chunks + 1, body, 0)

    def lw_copy(c):
        rows = pl.ds(pl.multiple_of(c * crow, 8), crow)
        return pltpu.make_async_remote_copy(
            lw.at[0, rows], lw_next.at[0, rows], lw_send.at[c], lw_recv.at[c], **at(low))

    def lw_rows(r):
        lw[0, pl.ds(r, ROWS), :] = lifted(0, r)

    chunked(lambda c: None, lw_rows, [(has_low, lambda c: lw_copy(c).start())])
    lax.fori_loop(0, nb, code_rows, 0)

    def z_copy(src, dst, send, recv, base, device):
        def copy(c):
            rows = pl.ds(pl.multiple_of(c * crow + PAD, 8), crow)
            return pltpu.make_async_remote_copy(
                z.at[src, rows], z.at[dst, rows], send.at[base + c], recv.at[base + c], **at(device))
        return copy

    down = [z_copy(2 + j, depth + 2 + j, dn_send, dn_recv, j * chunks, low) for j in range(2)]
    up = [z_copy(depth + j, j, up_send, up_recv, j * chunks, high) for j in range(2)]

    def z_rows(p, r):
        rows = pl.ds(r, ROWS)
        a = u[p, rows, :]
        flat = jnp.where(lane == nx - 1, 0.0, pltpu.roll(a, nx - 1, 1)) - a
        b = v[p, pl.ds(r, ROWS + PAD), :]
        flat = flat + (b[1 : ROWS + 1] - b[:ROWS])
        above = lifted(p + 1, r) if p + 1 < depth else lw_next[0, rows, :]
        own = lw[0, rows, :] if p == 0 else lifted(p, r)
        div = flat + (above - own)
        k = code[p + 1, rows, :]
        z[p + 2, pl.ds(pl.multiple_of(r + PAD, 8), ROWS), :] = (
            jnp.where(k >= 0.0, div, 0.0) / jnp.maximum(k, 1.0))

    def gated(before, copy):
        def start(c):
            before(c).wait_send()
            copy(c).start()
        return start

    top_plane = [] if depth > 2 else [(has_high, lambda c: up[0](c).start())]
    chunked(lambda c: None, functools.partial(z_rows, 0), top_plane)
    for p in range(1, depth - 1):
        sends = [(has_high, lambda c: up[0](c).start())] if p == depth - 2 else []
        chunked(lambda c: None, functools.partial(z_rows, p), sends)

    def above_wait(c):
        @pl.when(has_high)
        def _():
            lw_copy(c).wait_recv()

    chunked(above_wait, functools.partial(z_rows, depth - 1),
            [(has_high, gated(up[0], up[1])), (has_low, gated(lw_copy, down[0]))])

    def wait_all(cond, copy):
        def body(c, carry):
            @pl.when(cond)
            def _():
                copy(c).wait_recv()
            return carry
        lax.fori_loop(0, chunks, body, 0)

    def image(ref, slot, zm, zp, r, k):
        x = ref[slot, pl.ds(r, ROWS + 2 * PAD), :]
        mid = x[PAD : PAD + ROWS]
        beside = x[PAD + 1 : PAD + 1 + ROWS] + x[PAD - 1 : PAD - 1 + ROWS]
        beside = beside + jnp.where(lane == nx - 1, 0.0, pltpu.roll(mid, nx - 1, 1))
        beside = beside + jnp.where(lane == 0, 0.0, pltpu.roll(mid, 1, 1))
        beside = beside + zm + zp
        return mid, jnp.where(k >= 0.0, k * mid - beside, mid)

    def add(j, x):
        acc[j] += jnp.sum(x.reshape(ROWS // 8, 8, nx), axis=0)

    def y_rows(p, r):
        inner = pl.ds(pl.multiple_of(r + PAD, 8), ROWS)
        k = code[p + 1, pl.ds(r, ROWS), :]
        mid, q = image(z, p + 2, z[p + 1, inner, :], z[p + 3, inner, :], r, k)
        scaling = jnp.maximum(k, 1.0)
        out = q / scaling
        y[p + 1, inner, :] = out
        if 0 <= p < depth:
            d = scaling * mid
            add(0, d * mid)
            add(1, d * d)
            add(2, jnp.where(k >= 0.0, 1.0, 0.0))
            add(3, mid * q)
            add(4, q * out)

    def a_rows(p, r):
        inner = pl.ds(pl.multiple_of(r + PAD, 8), ROWS)
        k = code[p + 1, pl.ds(r, ROWS), :]
        mid, q = image(y, p + 1, y[p, inner, :], y[p + 2, inner, :], r, k)
        ay[p, pl.ds(r, ROWS), :] = q
        add(5, mid * q)

    def sweep(fn):
        def body(i, carry):
            fn(pl.multiple_of(i * ROWS, 8))
            return carry
        lax.fori_loop(0, nb, body, 0)

    for p in range(1, depth - 1):
        sweep(functools.partial(y_rows, p))
    wait_all(has_low, up[0])

    def push(c, carry):
        @pl.when(has_low)
        def _():
            gated(down[0], down[1])(c)
        return carry

    lax.fori_loop(0, chunks, push, 0)

    def middle(c, carry):
        def over(c, fn):
            def inner(i, k):
                fn(pl.multiple_of(c * crow + i * ROWS, 8))
                return k
            lax.fori_loop(0, crow // ROWS, inner, 0)

        def ahead(r):
            for p in sorted({0, depth - 1, depth}):
                y_rows(p, r)

        def behind(r):
            y_rows(-1, r)
            for p in range(depth):
                a_rows(p, r)

        @pl.when(c < chunks)
        def _():
            @pl.when(has_low)
            def _():
                up[1](c).wait_recv()

            @pl.when(has_high)
            def _():
                down[1](c).wait_recv()

                @pl.when(c == 0)
                def _():
                    down[0](0).wait_recv()

                @pl.when(c + 1 < chunks)
                def _():
                    down[0](c + 1).wait_recv()

            over(c, ahead)

        @pl.when(c > 0)
        def _():
            over(c - 1, behind)
        return carry

    lax.fori_loop(0, chunks + 1, middle, 0)

    for j in range(6):
        t = jnp.sum(acc[j], axis=0, keepdims=True)
        part = t[:, 0:128]
        for c in range(128, nx, 128):
            part = part + t[:, c : c + 128]
        st[j : j + 1, :] = part
    st[6:8, :] = jnp.zeros((2, 128), jnp.float32)
    st_start, st_wait = spread(st, st_all, st_send, st_recv)
    st_start()

    def drain(c, carry):
        @pl.when(has_low)
        def _():
            down[1](c).wait_send()

        @pl.when(has_high)
        def _():
            up[1](c).wait_send()
        return carry

    lax.fori_loop(0, chunks, drain, 0)
    st_wait()
    st_all[0] = st[...]
    total = jnp.sum(jnp.sum(st_all[...], axis=0), axis=1, keepdims=True)
    total = jnp.broadcast_to(total, (8, nx))
    gamma, squares, fluid = total[0:1], total[1:2], total[2:3]
    delta, eta, theta = total[3:4], total[4:5], total[5:6]
    alpha = gamma / delta
    gamma_next = gamma - 2.0 * alpha * delta + alpha * alpha * eta
    beta = gamma_next / gamma
    mixed = delta - alpha * eta
    curve = (delta - 2.0 * alpha * eta + alpha * alpha * theta) + 2.0 * beta * mixed + beta * beta * delta
    alpha_next = gamma_next / curve
    cf[1:2, :] = alpha + alpha_next * (1.0 + beta)
    cf[2:3, :] = alpha * alpha_next
    cf[3:4, :] = 1.0 / jnp.sqrt(squares / jnp.maximum(fluid, 1.0) + EPS)

    def out_copy(p, c, j):
        rows = pl.ds(pl.multiple_of(c * crow, 8), crow)
        src, dst = ((w, imp_hbm), (s, res_hbm))[j]
        return pltpu.make_async_copy(src.at[p, rows], dst.at[p, rows], out_sem.at[j * depth + p, c])

    for p in range(depth):
        def out_rows(r, p=p):
            inner = pl.ds(pl.multiple_of(r + PAD, 8), ROWS)
            rows = pl.ds(r, ROWS)
            zz, yy = z[p + 2, inner, :], y[p + 1, inner, :]
            scaling = jnp.maximum(code[p + 1, rows, :], 1.0)
            a, b = cf[1:2, :], cf[2:3, :]
            w[p, rows, :] = a * zz - b * yy
            s[p, rows, :] = (scaling * (zz - a * yy) + b * ay[p, rows, :]) * cf[3:4, :]

        chunked(lambda c: None, out_rows,
                [(True, lambda c, p=p: out_copy(p, c, 0).start()), (True, lambda c, p=p: out_copy(p, c, 1).start())])

    def finish(c, carry):
        for p in range(depth):
            for j in range(2):
                out_copy(p, c, j).wait()
        return carry

    lax.fori_loop(0, chunks, finish, 0)


def solution(mesh):
    n = mesh.shape["gz"]

    def local(u_face, v_face, w_face, smoke, obstacles):
        depth, ny, nx = u_face.shape
        nw = obstacles.shape[1]
        chunks = 8
        f32, i32 = jnp.float32, jnp.int32
        dma = pltpu.SemaphoreType.DMA
        any_spec = pl.BlockSpec(memory_space=pl.ANY)
        shape = jax.ShapeDtypeStruct((depth, ny, nx), f32)
        return pl.pallas_call(
            functools.partial(kernel, n, chunks),
            out_shape=(shape, shape),
            in_specs=[any_spec] * 5,
            out_specs=(any_spec, any_spec),
            scratch_shapes=[
                pltpu.VMEM((depth, ny, nx), f32),
                pltpu.VMEM((depth, ny + PAD, nx), f32),
                pltpu.VMEM((depth, ny, nx), f32),
                pltpu.VMEM((depth, ny, nx), f32),
                pltpu.VMEM((depth + 4, ny + 2 * PAD, nx), f32),
                pltpu.VMEM((depth + 2, ny + 2 * PAD, nx), f32),
                pltpu.VMEM((depth + 2, ny, nx), f32),
                pltpu.VMEM((depth, ny, nx), f32),
                pltpu.VMEM((1, ny, nx), f32),
                pltpu.VMEM((1, ny, nx), f32),
                pltpu.VMEM((depth + 4, nw, nx), i32),
                pltpu.VMEM((depth + 2, 4, nw, nx), i32),
                pltpu.VMEM((6, 8, nx), f32),
                pltpu.VMEM((8, nx), f32),
                pltpu.VMEM((8, 128), f32),
                pltpu.VMEM((n, 8, 128), f32),
                pltpu.VMEM((8, 128), f32),
                pltpu.VMEM((n, 8, 128), f32),
                dma((4 * depth + 1,)),
                dma((2,)), dma((2,)),
                dma((chunks,)), dma((chunks,)),
                dma((2 * chunks,)), dma((2 * chunks,)),
                dma((2 * chunks,)), dma((2 * chunks,)),
                dma((n,)), dma((n,)),
                dma((n,)), dma((n,)),
                dma((2 * depth, chunks)),
            ],
            compiler_params=pltpu.CompilerParams(
                collective_id=0, has_side_effects=True, vmem_limit_bytes=66_000_000),
            name="smoke_step",
        )(u_face, v_face, w_face, smoke, obstacles)

    placed = P("gz", None, None)
    return jax.shard_map(local, mesh=mesh, in_specs=(placed,) * 5, out_specs=(placed, placed), check_vma=False)
```

profile of v0, /device:TPU:1, one launch (start us, length us, event | category | flops | bytes accessed | tf_op | source)
XLA Modules:
  0.0 150.7 jit_solution(1673391535186870036)
XLA Ops:
  0.6 143.2 %smoke_step.1 = (f32[2,1024,512]{2,1,0:T(8,128)}, f32[2,1024,512]{2,1,0:T(8,128)}) custom-call(f32[2,1024,512]{2,1,0:T(8,128)} %u_hbm.1, f32[2,1024,512]{2,1,0:T(8,128)} %v_hbm.1, f32[2,1024,512]{2,1,0:T(8,128)} %w_hbm.1, f32[2,1024,512]{2,1,0:T(8,128)} %s_hbm.1, s32[2,32,512]{2,1,0:T(8,128)} %ob_hbm.1), custom_call_target="tpu_custom_call" | custom-call | tf_op jit(solution)/shard_map/smoke_step/pallas_call | solution.py:453
  143.9 0.0 copy-start
  143.9 4.8 %copy.9 = f32[2,1024,512]{2,1,0:T(8,128)} copy(f32[2,1024,512]{2,1,0:T(8,128)} %get-tuple-element.4) | data formatting | bytes 8388608
  148.7 0.0 copy-done
  148.7 2.0 %copy.10 = f32[2,1024,512]{2,1,0:T(8,128)} copy(f32[2,1024,512]{2,1,0:T(8,128)S(1)} %copy-done) | data formatting | bytes 8388608
Async XLA Ops:
  143.9 4.8 %copy-start = (f32[2,1024,512]{2,1,0:T(8,128)S(1)}, f32[2,1024,512]{2,1,0:T(8,128)}, u32[]{:S(2)}) copy-start(f32[2,1024,512]{2,1,0:T(8,128)} %get-tuple-element.5) | copy-start | bytes 12582916
where the time goes:
time: 151 us
  Pallas kernels  143 us (95%)
  local copies, waits for them, and re-layouts  6.84 us (5%)
    pallas_call x1, Pallas kernels, local(): pl.pallas_call(functools.partial(kernel, n, chunks), out_shape=(shape, sh...  143 us
    unnamed x4, local copies, waits for them, and re-layouts  6.84 us

commit v1 on v0

--- a/solution.py
+++ b/solution.py
@@ -15,10 +15,10 @@
 PAD = 8
 
 
-def kernel(n, chunks, u_hbm, v_hbm, w_hbm, s_hbm, ob_hbm, imp_hbm, res_hbm,
-           u, v, w, s, z, y, code, ay, lw, lw_next, ob, cw, acc, cf, mx, mx_all, st, st_all,
+def kernel(n, chunks, u_hbm, v_hbm, w_hbm, s_hbm, ob_hbm, w, s,
+           u, v, z, y, code, ay, lw, lw_next, ob, cw, acc, cf, mx, mx_all, st, st_all,
            in_sem, ob_send, ob_recv, lw_send, lw_recv, dn_send, dn_recv, up_send, up_recv,
-           mx_send, mx_recv, st_send, st_recv, out_sem):
+           mx_send, mx_recv, st_send, st_recv):
     depth, ny, nx = w.shape
     nb = ny // ROWS
     crow = ny // chunks
@@ -412,11 +412,6 @@
     cf[2:3, :] = alpha * alpha_next
     cf[3:4, :] = 1.0 / jnp.sqrt(squares / jnp.maximum(fluid, 1.0) + EPS)
 
-    def out_copy(p, c, j):
-        rows = pl.ds(pl.multiple_of(c * crow, 8), crow)
-        src, dst = ((w, imp_hbm), (s, res_hbm))[j]
-        return pltpu.make_async_copy(src.at[p, rows], dst.at[p, rows], out_sem.at[j * depth + p, c])
-
     for p in range(depth):
         def out_rows(r, p=p):
             inner = pl.ds(pl.multiple_of(r + PAD, 8), ROWS)
@@ -427,16 +422,7 @@
             w[p, rows, :] = a * zz - b * yy
             s[p, rows, :] = (scaling * (zz - a * yy) + b * ay[p, rows, :]) * cf[3:4, :]
 
-        chunked(lambda c: None, out_rows,
-                [(True, lambda c, p=p: out_copy(p, c, 0).start()), (True, lambda c, p=p: out_copy(p, c, 1).start())])
-
-    def finish(c, carry):
-        for p in range(depth):
-            for j in range(2):
-                out_copy(p, c, j).wait()
-        return carry
-
-    lax.fori_loop(0, chunks, finish, 0)
+        sweep(out_rows)
 
 
 def solution(mesh):
@@ -449,17 +435,16 @@
         f32, i32 = jnp.float32, jnp.int32
         dma = pltpu.SemaphoreType.DMA
         any_spec = pl.BlockSpec(memory_space=pl.ANY)
-        shape = jax.ShapeDtypeStruct((depth, ny, nx), f32)
+        shape = pltpu.VMEM((depth, ny, nx), f32)
+        vmem_spec = pl.BlockSpec(memory_space=pltpu.VMEM)
         return pl.pallas_call(
             functools.partial(kernel, n, chunks),
             out_shape=(shape, shape),
             in_specs=[any_spec] * 5,
-            out_specs=(any_spec, any_spec),
+            out_specs=(vmem_spec, vmem_spec),
             scratch_shapes=[
                 pltpu.VMEM((depth, ny, nx), f32),
                 pltpu.VMEM((depth, ny + PAD, nx), f32),
-                pltpu.VMEM((depth, ny, nx), f32),
-                pltpu.VMEM((depth, ny, nx), f32),
                 pltpu.VMEM((depth + 4, ny + 2 * PAD, nx), f32),
                 pltpu.VMEM((depth + 2, ny + 2 * PAD, nx), f32),
                 pltpu.VMEM((depth + 2, ny, nx), f32),
@@ -481,10 +466,9 @@
                 dma((2 * chunks,)), dma((2 * chunks,)),
                 dma((n,)), dma((n,)),
                 dma((n,)), dma((n,)),
-                dma((2 * depth, chunks)),
             ],
             compiler_params=pltpu.CompilerParams(
-                collective_id=0, has_side_effects=True, vmem_limit_bytes=66_000_000),
+                collective_id=0, has_side_effects=True, vmem_limit_bytes=58_000_000),
             name="smoke_step",
         )(u_face, v_face, w_face, smoke, obstacles)
 

time: 151 us -> 147 us (0.974)
  local copies, waits for them, and re-layouts: 6.84 us -> 4.03 us
  Pallas kernels: 143 us -> 141 us
    unnamed x4 -> x2, local copies, waits for them, and re-layouts: 6.84 us -> 4.03 us
    pallas_call x1, Pallas kernels: 143 us -> 141 us  [local(): pl.pallas_call(functools.partial(kernel, n, chunks), out_shape=(shape, sh...]
where the time goes in v1:
time: 147 us; the launch traced here: 146 us
  Pallas kernels  141 us (96%)
  local copies, waits for them, and re-layouts  4.03 us (3%)
    pallas_call x1, Pallas kernels, local(): pl.pallas_call(functools.partial(kernel, n, chunks), out_shape=(shape, sh...  141 us
    unnamed x2, local copies, waits for them, and re-layouts  4.03 us

profile of v1, /device:TPU:1, one launch (start us, length us, event | category | flops | bytes accessed | tf_op | source)
XLA Modules:
  0.0 146.0 jit_solution(15066607566661262901)
XLA Ops:
  0.6 141.3 %smoke_step.1 = (f32[2,1024,512]{2,1,0:T(8,128)S(1)}, f32[2,1024,512]{2,1,0:T(8,128)S(1)}) custom-call(f32[2,1024,512]{2,1,0:T(8,128)} %u_hbm.1, f32[2,1024,512]{2,1,0:T(8,128)} %v_hbm.1, f32[2,1024,512]{2,1,0:T(8,128)} %w_hbm.1, f32[2,1024,512]{2,1,0:T(8,128)} %s_hbm.1, s32[2,32,512]{2,1,0:T(8,128)} %ob_hbm.1), custom_call_target="tpu_custom_call" | custom-call | tf_op jit(solution)/shard_map/smoke_step/pallas_call | solution.py:440
  142.0 2.0 %copy.9 = f32[2,1024,512]{2,1,0:T(8,128)} copy(f32[2,1024,512]{2,1,0:T(8,128)S(1)} %get-tuple-element.2) | data formatting | bytes 8388608
  144.0 2.0 %copy.10 = f32[2,1024,512]{2,1,0:T(8,128)} copy(f32[2,1024,512]{2,1,0:T(8,128)S(1)} %get-tuple-element.3) | data formatting | bytes 8388608

commit v2 on v1

v2 whole, which is shorter than its diff:
```python
import functools

import jax
import jax.numpy as jnp
from jax import lax
from jax.experimental import pallas as pl
from jax.experimental.pallas import tpu as pltpu
from jax.sharding import PartitionSpec as P

EPS = 1e-06
CFL = 0.5
BUOYANCY = 100.0

ROWS = 32
PAD = 8


def kernel(n, chunks, raw, u_hbm, v_hbm, w_hbm, s_hbm, ob_hbm, w, s,
           u, v, z, y, code, inv, ay, lw, lw_next, s_next, ob, cw, acc, cf, mx, mx_all, st, st_pair, st_all, total,
           in_sem, ob_send, ob_recv, raw_send, raw_recv, lw_send, lw_recv, dn_send, dn_recv, up_send, up_recv,
           yd_send, yd_recv, mx_send, mx_recv, st_send, st_recv, pair_send, pair_recv):
    depth, ny, nx = w.shape
    top = depth - 1
    nb = ny // ROWS
    crow = ny // chunks
    me = lax.axis_index("gz")
    has_low, has_high = me > 0, me < n - 1
    low, high = jnp.maximum(me - 1, 0), jnp.minimum(me + 1, n - 1)
    odd = lax.rem(me, 2) == 1
    even = jnp.logical_not(odd)
    partner = me + 1 - 2 * lax.rem(me, 2)

    def at(device):
        return dict(device_id=(device,), device_id_type=pl.DeviceIdType.MESH)

    ins = [(u_hbm, u), (v_hbm, v), (w_hbm, w), (s_hbm, s)]

    def load(k, p, first=0, rows=ny, sem=None):
        src, dst = ins[k]
        part = pl.ds(first, rows)
        return pltpu.make_async_copy(src.at[p, part], dst.at[p, part], in_sem.at[k * depth + p if sem is None else sem])

    raw_rows = raw * crow
    ob_in = pltpu.make_async_copy(ob_hbm, ob.at[pl.ds(2, depth)], in_sem.at[4 * depth])
    raw_in = [load(k, 0, 0, raw_rows, 4 * depth + k - 1) for k in (2, 3)]
    rest_in = {(k, p): load(k, p, raw_rows, ny - raw_rows) if k >= 2 and p == 0 else load(k, p)
               for k in range(4) for p in range(depth)}
    ob_in.start()
    for copy in raw_in:
        copy.start()
    for copy in rest_in.values():
        copy.start()

    barrier = pltpu.get_barrier_semaphore()

    def greet(i, carry):
        pl.semaphore_signal(barrier, inc=1, **at(lax.rem(me + i, n)))
        return carry

    lax.fori_loop(1, n, greet, 0)

    zrow = jnp.zeros((PAD, nx), jnp.float32)
    for p in range(1, depth + 2):
        z[p, 0:PAD, :] = zrow
        z[p, ny + PAD : ny + 2 * PAD, :] = zrow
    for p in range(1, depth + 1):
        y[p, 0:PAD, :] = zrow
        y[p, ny + PAD : ny + 2 * PAD, :] = zrow
    for p in range(depth):
        v[p, ny : ny + PAD, :] = zrow
    acc[...] = jnp.zeros_like(acc)

    def zero_planes(ref, planes, offset):
        def body(i, carry):
            for p in planes:
                ref[p, pl.ds(pl.multiple_of(i * ROWS + offset, 8), ROWS), :] = jnp.zeros((ROWS, nx), jnp.float32)
            return carry
        lax.fori_loop(0, nb, body, 0)

    ob_in.wait()
    for copy in raw_in:
        copy.wait()
    pl.semaphore_wait(barrier, n - 1)

    ob_down = pltpu.make_async_remote_copy(
        ob.at[pl.ds(2, 1)], ob.at[pl.ds(depth + 2, 1)], ob_send.at[0], ob_recv.at[0], **at(low))
    ob_up = pltpu.make_async_remote_copy(
        ob.at[pl.ds(depth, 2)], ob.at[pl.ds(0, 2)], ob_send.at[1], ob_recv.at[1], **at(high))

    def raw_copies(c):
        rows = pl.ds(c * crow, crow)
        return [
            pltpu.make_async_remote_copy(
                src.at[0, rows], dst.at[0, rows], raw_send.at[2 * c + j], raw_recv.at[2 * c + j], **at(low))
            for j, (src, dst) in enumerate([(w, lw_next), (s, s_next)])
        ]

    def send_raw(first, last):
        @pl.when(has_low)
        def _():
            for c in range(first, last):
                for copy in raw_copies(c):
                    copy.start()

    @pl.when(has_low)
    def _():
        ob_down.start()

    @pl.when(has_high)
    def _():
        ob_up.start()

    send_raw(0, raw // 2)

    @pl.when(jnp.logical_not(has_low))
    def _():
        ob[0:2] = jnp.zeros((2,) + ob.shape[1:], jnp.int32)
        zero_planes(z, (0, 1), PAD)

    @pl.when(jnp.logical_not(has_high))
    def _():
        ob[depth + 2 : depth + 3] = jnp.zeros((1,) + ob.shape[1:], jnp.int32)
        zero_planes(z, (depth + 2,), PAD)
        zero_planes(lw_next, (0,), 0)

    peak = jnp.zeros((8, nx), jnp.float32)
    for k in range(3):
        ref = ins[k][1]
        for p in range(depth):
            rest_in[k, p].wait()

            def body(i, m, ref=ref, p=p):
                a = jnp.abs(ref[p, pl.ds(pl.multiple_of(i * ROWS, 8), ROWS), :])
                return jnp.maximum(m, jnp.max(a.reshape(ROWS // 8, 8, nx), axis=0))

            peak = lax.fori_loop(0, nb, body, peak)
    m = jnp.max(peak, axis=0, keepdims=True)
    part = m[:, 0:128]
    for c in range(128, nx, 128):
        part = jnp.maximum(part, m[:, c : c + 128])
    mx[...] = part

    def spread(src, dst, send, recv, step, count):
        def copy(i):
            return pltpu.make_async_remote_copy(
                src, dst.at[i], send.at[i], recv.at[i], **at(lax.rem(me + step * i, n)))

        def start(i, carry):
            copy(i).start()
            return carry

        def wait(i, carry):
            copy(i).wait_recv()
            copy(i).wait_send()
            return carry

        return (lambda: lax.fori_loop(1, count, start, 0)), (lambda: lax.fori_loop(1, count, wait, 0))

    mx_start, mx_wait = spread(mx, mx_all, mx_send, mx_recv, 1, n)
    mx_start()
    send_raw(raw // 2, raw)

    @pl.when(has_low)
    def _():
        ob_down.wait_send()
        ob_up.wait_recv()

    @pl.when(has_high)
    def _():
        ob_up.wait_send()
        ob_down.wait_recv()

    row_id = lax.broadcasted_iota(jnp.int32, (nb, nx), 0)
    col_id = lax.broadcasted_iota(jnp.int32, (nb, nx), 1)
    srl = lax.shift_right_logical
    c1, c31 = jnp.int32(1), jnp.int32(31)
    full1, full31 = jnp.full((nb, nx), c1), jnp.full((nb, nx), c31)
    for p in range(depth + 1):
        mid = ob[p + 1]
        after = jnp.where(row_id == nb - 1, 0, pltpu.roll(mid, nb - 1, 0))
        before = jnp.where(row_id == 0, 0, pltpu.roll(mid, 1, 0))
        a = srl(mid, full1) | (after << full31)
        b = (mid << full1) | srl(before, full31)
        c = jnp.where(col_id == nx - 1, 0, pltpu.roll(mid, nx - 1, 1))
        d = jnp.where(col_id == 0, 0, pltpu.roll(mid, 1, 1))
        e, f = ob[p], ob[p + 2]
        s1, k1 = a ^ b ^ c, (a & b) | (c & (a | b))
        s2, k2 = d ^ e ^ f, (d & e) | (f & (d | e))
        k3 = s1 & s2
        cw[p, 0] = s1 ^ s2
        cw[p, 1] = k1 ^ k2 ^ k3
        cw[p, 2] = (k1 & k2) | (k3 & (k1 | k2))
        cw[p, 3] = mid
    @pl.when(jnp.logical_not(has_low))
    def _():
        cw[0, 3] = jnp.full((nb, nx), -1, jnp.int32)

    half = 16
    places = lax.broadcasted_iota(jnp.int32, (half, nx), 0)

    def code_rows(b):
        for p in range(depth + 1):
            for k0 in range(0, ROWS, half):
                bits = [
                    srl(jnp.broadcast_to(cw[p, j, pl.ds(b, 1), :], (half, nx)), places + k0) & 1
                    for j in range(4)
                ]
                k = (6 - (bits[0] + (bits[1] << 1) + (bits[2] << 2))).astype(jnp.float32)
                rows = pl.ds(pl.multiple_of(b * ROWS + k0, 8), half)
                code[p, rows, :] = k
                inv[p, rows, :] = jnp.where(bits[3] == 1, 0.0, 1.0 / jnp.maximum(k, 1.0))

    for p in range(depth):
        rest_in[3, p].wait()
    mx_wait()
    mx_all[0] = mx[...]
    fastest = jnp.max(jnp.max(mx_all[...], axis=0), axis=1, keepdims=True)
    cf[0:1, :] = (CFL / (jnp.broadcast_to(fastest, (1, nx)) + EPS)) * BUOYANCY

    lane = lax.broadcasted_iota(jnp.int32, (ROWS, nx), 1)

    def lifted(p, r):
        rows = pl.ds(r, ROWS)
        return w[p, rows, :] + cf[0:1, :] * s[p, rows, :]

    def over(c, fn):
        def inner(i, k):
            fn(pl.multiple_of(c * crow + i * ROWS, 8))
            return k
        lax.fori_loop(0, crow // ROWS, inner, 0)

    def staged(first, second):
        def body(c, carry):
            @pl.when(c < chunks)
            def _():
                first(c)

            @pl.when(c > 0)
            def _():
                second(c - 1)
            return carry
        lax.fori_loop(0, chunks + 1, body, 0)

    def when(cond, fn):
        @pl.when(cond)
        def _():
            fn()

    def lw_copy(c):
        rows = pl.ds(pl.multiple_of(c * crow, 8), crow)
        return pltpu.make_async_remote_copy(
            lw.at[0, rows], lw_next.at[0, rows], lw_send.at[c], lw_recv.at[c], **at(low))

    def padded_copy(ref, src, dst, send, recv, base, device):
        def copy(c):
            rows = pl.ds(pl.multiple_of(c * crow + PAD, 8), crow)
            return pltpu.make_async_remote_copy(
                ref.at[src, rows], ref.at[dst, rows], send.at[base + c], recv.at[base + c], **at(device))
        return copy

    z_down = padded_copy(z, 2, depth + 2, dn_send, dn_recv, 0, low)
    top_up = padded_copy(z, top + 2, 1, up_send, up_recv, 0, high)
    next_up = padded_copy(z, top + 1, 0, up_send, up_recv, chunks, high)
    y_down = padded_copy(y, 1, depth + 1, yd_send, yd_recv, 0, low)

    def flat(p, r):
        a = u[p, pl.ds(r, ROWS), :]
        b = v[p, pl.ds(r, ROWS + PAD), :]
        return jnp.where(lane == nx - 1, 0.0, pltpu.roll(a, nx - 1, 1)) - a + (b[1 : ROWS + 1] - b[:ROWS])

    def inner_rows(r):
        return pl.ds(pl.multiple_of(r + PAD, 8), ROWS)

    def first_rows(r):
        code_rows(r // ROWS)
        rows = pl.ds(r, ROWS)
        lw[0, rows, :] = lifted(0, r)
        z[top + 2, inner_rows(r), :] = inv[top + 1, rows, :] * (flat(top, r) - lifted(top, r))

    def first_sends(c):
        when(jnp.logical_and(has_low, c >= raw), lambda: lw_copy(c).start())
        when(has_high, lambda: top_up(c).start())

    staged(lambda c: over(c, first_rows), first_sends)

    def z_rows(p, r):
        rows = pl.ds(r, ROWS)
        own = lw[0, rows, :] if p == 0 else lifted(p, r)
        z[p + 2, inner_rows(r), :] = inv[p + 1, rows, :] * (flat(p, r) + (lifted(p + 1, r) - own))

    for p in range(top):
        def z_sends(c, p=p):
            if p == 0:
                when(has_low, lambda: z_down(c).start())
            if p == top - 1:
                when(has_high, lambda: next_up(c).start())
        staged(lambda c, p=p: over(c, functools.partial(z_rows, p)), z_sends)

    @pl.when(has_high)
    def _():
        for c in range(raw):
            for copy in raw_copies(c):
                copy.wait_recv()

        def lift(i, carry):
            rows = pl.ds(pl.multiple_of(i * ROWS, 8), ROWS)
            lw_next[0, rows, :] = lw_next[0, rows, :] + cf[0:1, :] * s_next[0, rows, :]
            return carry

        lax.fori_loop(0, raw_rows // ROWS, lift, 0)

    def around(ref, slot, r):
        x = ref[slot, pl.ds(r, ROWS + 2 * PAD), :]
        mid = x[PAD : PAD + ROWS]
        beside = x[PAD + 1 : PAD + 1 + ROWS] + x[PAD - 1 : PAD - 1 + ROWS]
        beside = beside + jnp.where(lane == nx - 1, 0.0, pltpu.roll(mid, nx - 1, 1))
        beside = beside + jnp.where(lane == 0, 0.0, pltpu.roll(mid, 1, 1))
        return mid, beside

    def add(j, x):
        acc[j] += jnp.sum(x.reshape(ROWS // 8, 8, nx), axis=0)

    def y_rows(p, r):
        inner, rows = inner_rows(r), pl.ds(r, ROWS)
        k, scale = code[p + 1, rows, :], inv[p + 1, rows, :]
        mid, beside = around(z, p + 2, r)
        q = k * mid - (beside + z[p + 1, inner, :] + z[p + 3, inner, :])
        out = q * scale
        y[p + 1, inner, :] = out
        if p >= 0:
            d = jnp.maximum(k, 1.0) * mid
            add(0, d * mid)
            add(1, d * d)
            add(2, jnp.where(scale > 0.0, 1.0, 0.0))
            add(3, mid * q)
            add(4, q * out)

    def complete_rows(r):
        inner, rows = inner_rows(r), pl.ds(r, ROWS)
        z[top + 2, inner, :] = z[top + 2, inner, :] + inv[top + 1, rows, :] * lw_next[0, rows, :]
        z[1, inner, :] = z[1, inner, :] + inv[0, rows, :] * lw[0, rows, :]

    def low_rows(r):
        complete_rows(r)
        for p in range(top):
            y_rows(p, r)

    def low_chunk(c):
        @pl.when(has_high)
        def _():
            when(c >= raw, lambda: lw_copy(c).wait_recv())
            top_up(c).wait_send()

        when(has_low, lambda: top_up(c).wait_recv())
        over(c, low_rows)

    staged(low_chunk, lambda c: when(has_low, lambda: y_down(c).start()))

    def a_rows(p, r):
        inner, rows = inner_rows(r), pl.ds(r, ROWS)
        mid, beside = around(y, p + 1, r)
        below = y[p, inner, :]
        beside = beside + below
        if p < top:
            beside = beside + y[p + 2, inner, :]
        q = code[p + 1, rows, :] * mid - beside
        ay[p, rows, :] = jnp.where(inv[p + 1, rows, :] > 0.0, q, 0.0)
        add(5, mid * (q - below) if p == 0 else mid * q)

    def high_rows(r):
        y_rows(top, r)
        y_rows(-1, r)

    def high_chunk(c):
        when(has_high, lambda: z_down(c).wait_recv())
        when(has_low, lambda: next_up(c).wait_recv())
        over(c, high_rows)

    def image_rows(r):
        for p in range(depth):
            a_rows(p, r)

    staged(high_chunk, lambda c: over(c, image_rows))

    for j in range(6):
        t = jnp.sum(acc[j], axis=0, keepdims=True)
        part = t[:, 0:128]
        for c in range(128, nx, 128):
            part = part + t[:, c : c + 128]
        st[j : j + 1, :] = part
    st[6:8, :] = jnp.zeros((2, 128), jnp.float32)

    pair_in = pltpu.make_async_remote_copy(st, st_pair, pair_send.at[0], pair_recv.at[0], **at(partner))
    pair_out = pltpu.make_async_remote_copy(total, total, pair_send.at[1], pair_recv.at[1], **at(partner))
    st_start, st_wait = spread(st_pair, st_all, st_send, st_recv, 2, n // 2)

    @pl.when(even)
    def _():
        pair_in.start()

    @pl.when(odd)
    def _():
        pair_in.wait_recv()
        st_pair[...] = st_pair[...] + st[...]
        st_start()
        st_wait()
        st_all[0] = st_pair[...]
        total[...] = jnp.sum(st_all[...], axis=0)
        pair_out.start()

    @pl.when(has_low)
    def _():
        for c in range(raw):
            for copy in raw_copies(c):
                copy.wait_send()

    @pl.when(even)
    def _():
        pair_in.wait_send()
        pair_out.wait_recv()

    sums = jnp.broadcast_to(jnp.sum(total[...], axis=1, keepdims=True), (8, nx))
    gamma, squares, fluid = sums[0:1], sums[1:2], sums[2:3]
    delta, eta, theta = sums[3:4], sums[4:5], sums[5:6]
    alpha = gamma / delta
    gamma_next = gamma - 2.0 * alpha * delta + alpha * alpha * eta
    beta = gamma_next / gamma
    mixed = delta - alpha * eta
    curve = (delta - 2.0 * alpha * eta + alpha * alpha * theta) + 2.0 * beta * mixed + beta * beta * delta
    alpha_next = gamma_next / curve
    norm = 1.0 / jnp.sqrt(squares / jnp.maximum(fluid, 1.0) + EPS)
    cf[1:2, :] = alpha + alpha_next * (1.0 + beta)
    cf[2:3, :] = alpha * alpha_next
    cf[3:4, :] = norm
    cf[4:5, :] = alpha * alpha_next * norm

    def out_rows(r):
        inner, rows = inner_rows(r), pl.ds(r, ROWS)
        a, b = cf[1:2, :], cf[2:3, :]
        for p in range(depth):
            zz, yy = z[p + 2, inner, :], y[p + 1, inner, :]
            w[p, rows, :] = a * zz - b * yy
            s[p, rows, :] = (
                jnp.maximum(code[p + 1, rows, :], 1.0) * (zz - a * yy) + b * ay[p, rows, :]) * cf[3:4, :]

    def all_rows(i, carry):
        out_rows(pl.multiple_of(i * ROWS, 8))
        return carry

    lax.fori_loop(0, nb, all_rows, 0)

    def last_rows(r):
        inner, rows = inner_rows(r), pl.ds(r, ROWS)
        s[top, rows, :] = s[top, rows, :] - jnp.where(
            inv[top + 1, rows, :] > 0.0, cf[4:5, :] * y[depth + 1, inner, :], 0.0)

    @pl.when(has_high)
    def _():
        def last_chunk(c, carry):
            y_down(c).wait_recv()
            over(c, last_rows)
            return carry
        lax.fori_loop(0, chunks, last_chunk, 0)

    @pl.when(odd)
    def _():
        pair_out.wait_send()

    def drain(c, carry):
        @pl.when(has_low)
        def _():
            when(c >= raw, lambda: lw_copy(c).wait_send())
            z_down(c).wait_send()
            y_down(c).wait_send()

        when(has_high, lambda: next_up(c).wait_send())
        return carry

    lax.fori_loop(0, chunks, drain, 0)


def solution(mesh):
    n = mesh.shape["gz"]

    def local(u_face, v_face, w_face, smoke, obstacles):
        depth, ny, nx = u_face.shape
        nw = obstacles.shape[1]
        chunks, raw = 16, 2
        crow = ny // chunks
        f32, i32 = jnp.float32, jnp.int32
        dma = pltpu.SemaphoreType.DMA
        any_spec = pl.BlockSpec(memory_space=pl.ANY)
        vmem_spec = pl.BlockSpec(memory_space=pltpu.VMEM)
        shape = pltpu.VMEM((depth, ny, nx), f32)
        return pl.pallas_call(
            functools.partial(kernel, n, chunks, raw),
            out_shape=(shape, shape),
            in_specs=[any_spec] * 5,
            out_specs=(vmem_spec, vmem_spec),
            scratch_shapes=[
                pltpu.VMEM((depth, ny, nx), f32),
                pltpu.VMEM((depth, ny + PAD, nx), f32),
                pltpu.VMEM((depth + 3, ny + 2 * PAD, nx), f32),
                pltpu.VMEM((depth + 2, ny + 2 * PAD, nx), f32),
                pltpu.VMEM((depth + 1, ny, nx), f32),
                pltpu.VMEM((depth + 1, ny, nx), f32),
                pltpu.VMEM((depth, ny, nx), f32),
                pltpu.VMEM((1, ny, nx), f32),
                pltpu.VMEM((1, ny, nx), f32),
                pltpu.VMEM((1, raw * crow, nx), f32),
                pltpu.VMEM((depth + 3, nw, nx), i32),
                pltpu.VMEM((depth + 1, 4, nw, nx), i32),
                pltpu.VMEM((6, 8, nx), f32),
                pltpu.VMEM((8, nx), f32),
                pltpu.VMEM((1, 128), f32),
                pltpu.VMEM((n, 1, 128), f32),
                pltpu.VMEM((8, 128), f32),
                pltpu.VMEM((8, 128), f32),
                pltpu.VMEM((n // 2, 8, 128), f32),
                pltpu.VMEM((8, 128), f32),
                dma((4 * depth + 3,)),
                dma((2,)), dma((2,)),
                dma((2 * raw,)), dma((2 * raw,)),
                dma((chunks,)), dma((chunks,)),
                dma((chunks,)), dma((chunks,)),
                dma((2 * chunks,)), dma((2 * chunks,)),
                dma((chunks,)), dma((chunks,)),
                dma((n,)), dma((n,)),
                dma((n // 2,)), dma((n // 2,)),
                dma((2,)), dma((2,)),
            ],
            compiler_params=pltpu.CompilerParams(
                collective_id=0, has_side_effects=True, vmem_limit_bytes=58_000_000),
            name="smoke_step",
        )(u_face, v_face, w_face, smoke, obstacles)

    placed = P("gz", None, None)
    return jax.shard_map(local, mesh=mesh, in_specs=(placed,) * 5, out_specs=(placed, placed), check_vma=False)
```

time: 147 us -> 143 us (0.973)
  Pallas kernels: 141 us -> 137 us
    pallas_call x1, Pallas kernels: 141 us -> 137 us  [local(): pl.pallas_call(functools.partial(kernel, n, chunks, raw), out_shape=(shap...]
where the time goes in v2:
time: 143 us; the launch traced here: 142 us
  Pallas kernels  137 us (96%)
  local copies, waits for them, and re-layouts  4.03 us (3%)
    pallas_call x1, Pallas kernels, local(): pl.pallas_call(functools.partial(kernel, n, chunks, raw), out_shape=(shap...  137 us
    unnamed x2, local copies, waits for them, and re-layouts  4.03 us

profile of v2, /device:TPU:1, one launch (start us, length us, event | category | flops | bytes accessed | tf_op | source)
XLA Modules:
  0.0 141.8 jit_solution(13431365399298660444)
XLA Ops:
  0.6 137.1 %smoke_step.1 = (f32[2,1024,512]{2,1,0:T(8,128)S(1)}, f32[2,1024,512]{2,1,0:T(8,128)S(1)}) custom-call(f32[2,1024,512]{2,1,0:T(8,128)} %u_hbm.1, f32[2,1024,512]{2,1,0:T(8,128)} %v_hbm.1, f32[2,1024,512]{2,1,0:T(8,128)} %w_hbm.1, f32[2,1024,512]{2,1,0:T(8,128)} %s_hbm.1, s32[2,32,512]{2,1,0:T(8,128)} %ob_hbm.1), custom_call_target="tpu_custom_call" | custom-call | tf_op jit(solution)/shard_map/smoke_step/pallas_call | solution.py:495
  137.7 2.0 %copy.9 = f32[2,1024,512]{2,1,0:T(8,128)} copy(f32[2,1024,512]{2,1,0:T(8,128)S(1)} %get-tuple-element.2) | data formatting | bytes 8388608
  139.7 2.0 %copy.10 = f32[2,1024,512]{2,1,0:T(8,128)} copy(f32[2,1024,512]{2,1,0:T(8,128)S(1)} %get-tuple-element.3) | data formatting | bytes 8388608

commit v3 on v2

--- a/solution.py
+++ b/solution.py
@@ -13,22 +13,29 @@
 
 ROWS = 32
 PAD = 8
-
-
-def kernel(n, chunks, raw, u_hbm, v_hbm, w_hbm, s_hbm, ob_hbm, w, s,
-           u, v, z, y, code, inv, ay, lw, lw_next, s_next, ob, cw, acc, cf, mx, mx_all, st, st_pair, st_all, total,
-           in_sem, ob_send, ob_recv, raw_send, raw_recv, lw_send, lw_recv, dn_send, dn_recv, up_send, up_recv,
-           yd_send, yd_recv, mx_send, mx_recv, st_send, st_recv, pair_send, pair_recv):
+SPAN = 8
+LEAD = 4
+
+
+def kernel(n, chunks, group, raw, u_hbm, v_hbm, w_hbm, s_hbm, ob_hbm, w, s,
+           u, v, z, part_z, y, code, inv, ay, lw, lw_next, s_next, ob, cw, acc, cf, mx, mx_all, st, st_pair, st_all, total,
+           in_sem, ob_send, ob_recv, raw_send, raw_recv, send, lw_recv, dn_recv, yd_recv, top_recv, next_recv,
+           mx_send, mx_recv, st_send, st_recv, pair_send, pair_recv, gate):
     depth, ny, nx = w.shape
     top = depth - 1
     nb = ny // ROWS
     crow = ny // chunks
+    grow = crow * group
+    groups = chunks // group
     me = lax.axis_index("gz")
     has_low, has_high = me > 0, me < n - 1
     low, high = jnp.maximum(me - 1, 0), jnp.minimum(me + 1, n - 1)
     odd = lax.rem(me, 2) == 1
     even = jnp.logical_not(odd)
     partner = me + 1 - 2 * lax.rem(me, 2)
+    place = lax.rem(me, SPAN)
+    gated = jnp.logical_and(has_low, place == 0)
+    gating = jnp.logical_and(place == 2, me + SPAN - 2 < n)
 
     def at(device):
         return dict(device_id=(device,), device_id_type=pl.DeviceIdType.MESH)
@@ -48,8 +55,9 @@
     ob_in.start()
     for copy in raw_in:
         copy.start()
-    for copy in rest_in.values():
-        copy.start()
+    for (k, _), copy in rest_in.items():
+        if k < 3:
+            copy.start()
 
     barrier = pltpu.get_barrier_semaphore()
 
@@ -87,20 +95,12 @@
     ob_up = pltpu.make_async_remote_copy(
         ob.at[pl.ds(depth, 2)], ob.at[pl.ds(0, 2)], ob_send.at[1], ob_recv.at[1], **at(high))
 
-    def raw_copies(c):
-        rows = pl.ds(c * crow, crow)
-        return [
-            pltpu.make_async_remote_copy(
-                src.at[0, rows], dst.at[0, rows], raw_send.at[2 * c + j], raw_recv.at[2 * c + j], **at(low))
-            for j, (src, dst) in enumerate([(w, lw_next), (s, s_next)])
-        ]
-
-    def send_raw(first, last):
-        @pl.when(has_low)
-        def _():
-            for c in range(first, last):
-                for copy in raw_copies(c):
-                    copy.start()
+    raw_part = pl.ds(0, raw_rows)
+    raw_copies = [
+        pltpu.make_async_remote_copy(
+            src.at[0, raw_part], dst.at[0, raw_part], raw_send.at[j], raw_recv.at[j], **at(low))
+        for j, (src, dst) in enumerate([(w, lw_next), (s, s_next)])
+    ]
 
     @pl.when(has_low)
     def _():
@@ -109,8 +109,6 @@
     @pl.when(has_high)
     def _():
         ob_up.start()
-
-    send_raw(0, raw // 2)
 
     @pl.when(jnp.logical_not(has_low))
     def _():
@@ -128,6 +126,8 @@
         ref = ins[k][1]
         for p in range(depth):
             rest_in[k, p].wait()
+            if k == 1:
+                rest_in[3, p].start()
 
             def body(i, m, ref=ref, p=p):
                 a = jnp.abs(ref[p, pl.ds(pl.multiple_of(i * ROWS, 8), ROWS), :])
@@ -141,24 +141,22 @@
     mx[...] = part
 
     def spread(src, dst, send, recv, step, count):
-        def copy(i):
-            return pltpu.make_async_remote_copy(
-                src, dst.at[i], send.at[i], recv.at[i], **at(lax.rem(me + step * i, n)))
-
         def start(i, carry):
-            copy(i).start()
+            pltpu.make_async_remote_copy(
+                src, dst.at[i], send, recv, **at(lax.rem(me + step * i, n))).start()
             return carry
 
-        def wait(i, carry):
-            copy(i).wait_recv()
-            copy(i).wait_send()
-            return carry
-
-        return (lambda: lax.fori_loop(1, count, start, 0)), (lambda: lax.fori_loop(1, count, wait, 0))
-
-    mx_start, mx_wait = spread(mx, mx_all, mx_send, mx_recv, 1, n)
+        everything = dst.at[pl.ds(1, count - 1)]
+        whole = pltpu.make_async_remote_copy(everything, everything, send, recv, **at(lax.rem(me + step, n)))
+        return (lambda: lax.fori_loop(1, count, start, 0)), whole
+
+    mx_start, mx_whole = spread(mx, mx_all, mx_send, mx_recv, 1, n)
     mx_start()
-    send_raw(raw // 2, raw)
+
+    @pl.when(has_low)
+    def _():
+        for copy in raw_copies:
+            copy.start()
 
     @pl.when(has_low)
     def _():
@@ -212,7 +210,7 @@
 
     for p in range(depth):
         rest_in[3, p].wait()
-    mx_wait()
+    mx_whole.wait_recv()
     mx_all[0] = mx[...]
     fastest = jnp.max(jnp.max(mx_all[...], axis=0), axis=1, keepdims=True)
     cf[0:1, :] = (CFL / (jnp.broadcast_to(fastest, (1, nx)) + EPS)) * BUOYANCY
@@ -223,15 +221,15 @@
         rows = pl.ds(r, ROWS)
         return w[p, rows, :] + cf[0:1, :] * s[p, rows, :]
 
-    def over(c, fn):
+    def over(c, fn, rows=crow):
         def inner(i, k):
-            fn(pl.multiple_of(c * crow + i * ROWS, 8))
+            fn(pl.multiple_of(c * rows + i * ROWS, 8))
             return k
-        lax.fori_loop(0, crow // ROWS, inner, 0)
-
-    def staged(first, second):
+        lax.fori_loop(0, rows // ROWS, inner, 0)
+
+    def staged(first, second, count=chunks):
         def body(c, carry):
-            @pl.when(c < chunks)
+            @pl.when(c < count)
             def _():
                 first(c)
 
@@ -239,29 +237,30 @@
             def _():
                 second(c - 1)
             return carry
-        lax.fori_loop(0, chunks + 1, body, 0)
+        lax.fori_loop(0, count + 1, body, 0)
 
     def when(cond, fn):
         @pl.when(cond)
         def _():
             fn()
 
-    def lw_copy(c):
-        rows = pl.ds(pl.multiple_of(c * crow, 8), crow)
-        return pltpu.make_async_remote_copy(
-            lw.at[0, rows], lw_next.at[0, rows], lw_send.at[c], lw_recv.at[c], **at(low))
-
-    def padded_copy(ref, src, dst, send, recv, base, device):
-        def copy(c):
-            rows = pl.ds(pl.multiple_of(c * crow + PAD, 8), crow)
-            return pltpu.make_async_remote_copy(
-                ref.at[src, rows], ref.at[dst, rows], send.at[base + c], recv.at[base + c], **at(device))
-        return copy
-
-    z_down = padded_copy(z, 2, depth + 2, dn_send, dn_recv, 0, low)
-    top_up = padded_copy(z, top + 2, 1, up_send, up_recv, 0, high)
-    next_up = padded_copy(z, top + 1, 0, up_send, up_recv, chunks, high)
-    y_down = padded_copy(y, 1, depth + 1, yd_send, yd_recv, 0, low)
+    class Flow:
+        def __init__(self, src, dst, send, recv, device, per, src_pad=PAD, dst_pad=PAD, first=0):
+            def copy(start, rows, index):
+                def part(pad):
+                    return pl.ds(pl.multiple_of(start + pad, 8), rows)
+                return pltpu.make_async_remote_copy(
+                    src[0].at[src[1], part(src_pad)], dst[0].at[dst[1], part(dst_pad)], send, recv.at[index], **at(device))
+
+            self.start = lambda c: copy(c * crow, crow, c // per).start()
+            self.wait_recv = lambda i: copy(i * crow * per, crow * per, i).wait_recv()
+            self.wait_send = lambda: copy(first, ny - first, 0).wait_send()
+
+    lw_down = Flow((lw, 0), (lw_next, 0), send.at[0], lw_recv, low, group, 0, 0, raw_rows)
+    z_down = Flow((z, 2), (z, depth + 2), send.at[1], dn_recv, low, group)
+    y_down = Flow((y, 1), (y, depth + 1), send.at[2], yd_recv, low, group)
+    top_up = Flow((part_z, 0), (z, 1), send.at[3], top_recv, high, group, 0)
+    next_up = Flow((z, top + 1), (z, 0), send.at[4], next_recv, high, 1)
 
     def flat(p, r):
         a = u[p, pl.ds(r, ROWS), :]
@@ -275,11 +274,11 @@
         code_rows(r // ROWS)
         rows = pl.ds(r, ROWS)
         lw[0, rows, :] = lifted(0, r)
-        z[top + 2, inner_rows(r), :] = inv[top + 1, rows, :] * (flat(top, r) - lifted(top, r))
+        part_z[0, rows, :] = inv[top + 1, rows, :] * (flat(top, r) - lifted(top, r))
 
     def first_sends(c):
-        when(jnp.logical_and(has_low, c >= raw), lambda: lw_copy(c).start())
-        when(has_high, lambda: top_up(c).start())
+        when(jnp.logical_and(has_low, c >= raw), lambda: lw_down.start(c))
+        when(has_high, lambda: top_up.start(c))
 
     staged(lambda c: over(c, first_rows), first_sends)
 
@@ -291,16 +290,15 @@
     for p in range(top):
         def z_sends(c, p=p):
             if p == 0:
-                when(has_low, lambda: z_down(c).start())
+                when(has_low, lambda: z_down.start(c))
             if p == top - 1:
-                when(has_high, lambda: next_up(c).start())
+                when(has_high, lambda: next_up.start(c))
         staged(lambda c, p=p: over(c, functools.partial(z_rows, p)), z_sends)
 
     @pl.when(has_high)
     def _():
-        for c in range(raw):
-            for copy in raw_copies(c):
-                copy.wait_recv()
+        for copy in raw_copies:
+            copy.wait_recv()
 
         def lift(i, carry):
             rows = pl.ds(pl.multiple_of(i * ROWS, 8), ROWS)
@@ -337,7 +335,7 @@
 
     def complete_rows(r):
         inner, rows = inner_rows(r), pl.ds(r, ROWS)
-        z[top + 2, inner, :] = z[top + 2, inner, :] + inv[top + 1, rows, :] * lw_next[0, rows, :]
+        z[top + 2, inner, :] = part_z[0, rows, :] + inv[top + 1, rows, :] * lw_next[0, rows, :]
         z[1, inner, :] = z[1, inner, :] + inv[0, rows, :] * lw[0, rows, :]
 
     def low_rows(r):
@@ -346,15 +344,15 @@
             y_rows(p, r)
 
     def low_chunk(c):
-        @pl.when(has_high)
-        def _():
-            when(c >= raw, lambda: lw_copy(c).wait_recv())
-            top_up(c).wait_send()
-
-        when(has_low, lambda: top_up(c).wait_recv())
-        over(c, low_rows)
-
-    staged(low_chunk, lambda c: when(has_low, lambda: y_down(c).start()))
+        when(jnp.logical_and(has_high, c >= raw // group), lambda: lw_down.wait_recv(c))
+        when(has_low, lambda: top_up.wait_recv(c))
+        over(c, low_rows, grow)
+
+    def start_y(c):
+        for i in range(group):
+            y_down.start(c * group + i)
+
+    staged(low_chunk, lambda c: when(jnp.logical_and(has_low, jnp.logical_not(gated)), lambda: start_y(c)), groups)
 
     def a_rows(p, r):
         inner, rows = inner_rows(r), pl.ds(r, ROWS)
@@ -372,15 +370,29 @@
         y_rows(-1, r)
 
     def high_chunk(c):
-        when(has_high, lambda: z_down(c).wait_recv())
-        when(has_low, lambda: next_up(c).wait_recv())
-        over(c, high_rows)
+        when(has_high, lambda: z_down.wait_recv(c))
+        for i in range(group):
+            chunk = c * group + i
+            when(has_low, lambda: next_up.wait_recv(chunk))
+            when(jnp.logical_and(gating, chunk == chunks - LEAD), lambda: pl.semaphore_signal(
+                gate, inc=1, **at(jnp.minimum(me + SPAN - 2, n - 1))))
+        over(c, high_rows, grow)
 
     def image_rows(r):
         for p in range(depth):
             a_rows(p, r)
 
-    staged(high_chunk, lambda c: over(c, image_rows))
+    staged(high_chunk, lambda c: over(c, image_rows, grow), groups)
+
+    @pl.when(gated)
+    def _():
+        pl.semaphore_wait(gate, 1)
+
+        def start(c, carry):
+            start_y(c)
+            return carry
+
+        lax.fori_loop(0, groups, start, 0)
 
     for j in range(6):
         t = jnp.sum(acc[j], axis=0, keepdims=True)
@@ -392,7 +404,7 @@
 
     pair_in = pltpu.make_async_remote_copy(st, st_pair, pair_send.at[0], pair_recv.at[0], **at(partner))
     pair_out = pltpu.make_async_remote_copy(total, total, pair_send.at[1], pair_recv.at[1], **at(partner))
-    st_start, st_wait = spread(st_pair, st_all, st_send, st_recv, 2, n // 2)
+    st_start, st_whole = spread(st_pair, st_all, st_send, st_recv, 2, n // 2)
 
     @pl.when(even)
     def _():
@@ -403,16 +415,15 @@
         pair_in.wait_recv()
         st_pair[...] = st_pair[...] + st[...]
         st_start()
-        st_wait()
+        st_whole.wait_recv()
         st_all[0] = st_pair[...]
         total[...] = jnp.sum(st_all[...], axis=0)
         pair_out.start()
 
     @pl.when(has_low)
     def _():
-        for c in range(raw):
-            for copy in raw_copies(c):
-                copy.wait_send()
+        for copy in raw_copies:
+            copy.wait_send()
 
     @pl.when(even)
     def _():
@@ -457,26 +468,38 @@
     @pl.when(has_high)
     def _():
         def last_chunk(c, carry):
-            y_down(c).wait_recv()
-            over(c, last_rows)
+            y_down.wait_recv(c)
+            over(c, last_rows, grow)
             return carry
-        lax.fori_loop(0, chunks, last_chunk, 0)
+        lax.fori_loop(0, groups, last_chunk, 0)
 
     @pl.when(odd)
     def _():
+        st_whole.wait_send()
         pair_out.wait_send()
 
-    def drain(c, carry):
-        @pl.when(has_low)
-        def _():
-            when(c >= raw, lambda: lw_copy(c).wait_send())
-            z_down(c).wait_send()
-            y_down(c).wait_send()
-
-        when(has_high, lambda: next_up(c).wait_send())
-        return carry
-
-    lax.fori_loop(0, chunks, drain, 0)
+    @pl.when(has_low)
+    def _():
+        for flow in (lw_down, z_down, y_down):
+            flow.wait_send()
+
+    @pl.when(has_high)
+    def _():
+        for flow in (top_up, next_up):
+            flow.wait_send()
+
+    mx_whole.wait_send()
+
+
+def store(w, s, w_hbm, s_hbm, sem):
+    copies = [
+        pltpu.make_async_copy(src.at[p], dst.at[p], sem.at[j, p])
+        for j, (src, dst) in enumerate([(w, w_hbm), (s, s_hbm)]) for p in range(w.shape[0])
+    ]
+    for copy in copies:
+        copy.start()
+    for copy in copies:
+        copy.wait()
 
 
 def solution(mesh):
@@ -485,15 +508,15 @@
     def local(u_face, v_face, w_face, smoke, obstacles):
         depth, ny, nx = u_face.shape
         nw = obstacles.shape[1]
-        chunks, raw = 16, 2
+        chunks, group, raw = 16, 2, 2
         crow = ny // chunks
         f32, i32 = jnp.float32, jnp.int32
         dma = pltpu.SemaphoreType.DMA
         any_spec = pl.BlockSpec(memory_space=pl.ANY)
         vmem_spec = pl.BlockSpec(memory_space=pltpu.VMEM)
         shape = pltpu.VMEM((depth, ny, nx), f32)
-        return pl.pallas_call(
-            functools.partial(kernel, n, chunks, raw),
+        results = pl.pallas_call(
+            functools.partial(kernel, n, chunks, group, raw),
             out_shape=(shape, shape),
             in_specs=[any_spec] * 5,
             out_specs=(vmem_spec, vmem_spec),
@@ -501,6 +524,7 @@
                 pltpu.VMEM((depth, ny, nx), f32),
                 pltpu.VMEM((depth, ny + PAD, nx), f32),
                 pltpu.VMEM((depth + 3, ny + 2 * PAD, nx), f32),
+                pltpu.VMEM((1, ny, nx), f32),
                 pltpu.VMEM((depth + 2, ny + 2 * PAD, nx), f32),
                 pltpu.VMEM((depth + 1, ny, nx), f32),
                 pltpu.VMEM((depth + 1, ny, nx), f32),
@@ -520,19 +544,28 @@
                 pltpu.VMEM((8, 128), f32),
                 dma((4 * depth + 3,)),
                 dma((2,)), dma((2,)),
-                dma((2 * raw,)), dma((2 * raw,)),
-                dma((chunks,)), dma((chunks,)),
-                dma((chunks,)), dma((chunks,)),
-                dma((2 * chunks,)), dma((2 * chunks,)),
-                dma((chunks,)), dma((chunks,)),
-                dma((n,)), dma((n,)),
-                dma((n // 2,)), dma((n // 2,)),
                 dma((2,)), dma((2,)),
+                dma((5,)),
+                dma((chunks // group,)), dma((chunks // group,)), dma((chunks // group,)), dma((chunks // group,)),
+                dma((chunks,)),
+                dma, dma, dma, dma,
+                dma((2,)), dma((2,)),
+                pltpu.SemaphoreType.REGULAR,
             ],
             compiler_params=pltpu.CompilerParams(
                 collective_id=0, has_side_effects=True, vmem_limit_bytes=58_000_000),
             name="smoke_step",
         )(u_face, v_face, w_face, smoke, obstacles)
+        out = jax.ShapeDtypeStruct((depth, ny, nx), f32)
+        return pl.pallas_call(
+            store,
+            out_shape=(out, out),
+            in_specs=[vmem_spec] * 2,
+            out_specs=(any_spec, any_spec),
+            scratch_shapes=[dma((2, depth))],
+            compiler_params=pltpu.CompilerParams(vmem_limit_bytes=1_000_000),
+            name="store",
+        )(*results)
 
     placed = P("gz", None, None)
     return jax.shard_map(local, mesh=mesh, in_specs=(placed,) * 5, out_specs=(placed, placed), check_vma=False)

time: 143 us -> 131 us (0.916)
  Pallas kernels: 137 us -> 130 us
  local copies, waits for them, and re-layouts: 4.03 us -> 0 us
    pallas_call x1 -> x2, Pallas kernels: 137 us -> 130 us  [the longest x1 127 us: local(): pl.pallas_call(functools.partial(kernel, n, chunks, group, raw), out_shap...]
    unnamed x2 -> x0, local copies, waits for them, and re-layouts: 4.03 us -> none
where the time goes in v3:
time: 131 us
  Pallas kernels  130 us (99%)
    pallas_call x1, Pallas kernels, local(): pl.pallas_call(functools.partial(kernel, n, chunks, group, raw), out_shap...  127 us
    pallas_call x1, Pallas kernels, local(): pl.pallas_call(store, out_shape=(out, out), in_specs=[vmem_spec] * 2, out...  3.37 us

profile of v3, /device:TPU:1, one launch (start us, length us, event | category | flops | bytes accessed | tf_op | source)
XLA Modules:
  0.0 130.8 jit_solution(1360331422623425193)
XLA Ops:
  0.6 126.8 %smoke_step.1 = (f32[2,1024,512]{2,1,0:T(8,128)S(1)}, f32[2,1024,512]{2,1,0:T(8,128)S(1)}) custom-call(f32[2,1024,512]{2,1,0:T(8,128)} %u_hbm.1, f32[2,1024,512]{2,1,0:T(8,128)} %v_hbm.1, f32[2,1024,512]{2,1,0:T(8,128)} %w_hbm.1, f32[2,1024,512]{2,1,0:T(8,128)} %s_hbm.1, s32[2,32,512]{2,1,0:T(8,128)} %ob_hbm.1), custom_call_target="tpu_custom_call" | custom-call | tf_op jit(solution)/shard_map/smoke_step/pallas_call | solution.py:518
  127.4 3.4 %store.1 = (f32[2,1024,512]{2,1,0:T(8,128)}, f32[2,1024,512]{2,1,0:T(8,128)}) custom-call(f32[2,1024,512]{2,1,0:T(8,128)S(1)} %get-tuple-element.4.w, f32[2,1024,512]{2,1,0:T(8,128)S(1)} %get-tuple-element.5.s), custom_call_target="tpu_custom_call" | custom-call | tf_op jit(solution)/shard_map/store/pallas_call | solution.py:560

commit v4 on v3

--- a/solution.py
+++ b/solution.py
@@ -15,11 +15,12 @@
 PAD = 8
 SPAN = 8
 LEAD = 4
+OPEN = 5
 
 
 def kernel(n, chunks, group, raw, u_hbm, v_hbm, w_hbm, s_hbm, ob_hbm, w, s,
-           u, v, z, part_z, y, code, inv, ay, lw, lw_next, s_next, ob, cw, acc, cf, mx, mx_all, st, st_pair, st_all, total,
-           in_sem, ob_send, ob_recv, raw_send, raw_recv, send, lw_recv, dn_recv, yd_recv, top_recv, next_recv,
+           u, v, z, part_z, y, code, inv, ay, lw, lw_next, s_next, relay, ob, cw, acc, cf, mx, mx_all, st, st_pair, st_all, total,
+           in_sem, ob_send, ob_recv, raw_send, raw_recv, send, lw_recv, dn_recv, yd_recv, top_recv, next_recv, relay_recv, relay_send,
            mx_send, mx_recv, st_send, st_recv, pair_send, pair_recv, gate):
     depth, ny, nx = w.shape
     top = depth - 1
@@ -36,6 +37,46 @@
     place = lax.rem(me, SPAN)
     gated = jnp.logical_and(has_low, place == 0)
     gating = jnp.logical_and(place == 2, me + SPAN - 2 < n)
+
+    span, spans = me // SPAN, n // SPAN
+    plane_units = groups
+    head = plane_units // 2
+    few = plane_units // 4
+    every = head + plane_units
+
+    def piece(count):
+        return head - jnp.maximum(count - plane_units, 0), head + jnp.minimum(count, plane_units)
+
+    def select(cases):
+        first, last = 0, 0
+        for cond, (lo, hi) in cases:
+            first, last = jnp.where(cond, lo, first), jnp.where(cond, hi, last)
+        return first, last
+
+    def cross_up(lower):
+        return piece(jnp.minimum(head * (spans - 1 - lower), every))
+
+    def cross_down(upper):
+        return piece(jnp.minimum(head * upper, every))
+
+    side = (every - few, every)
+    whole_spans = n % SPAN == 0
+    crossing = jnp.logical_and(whole_spans, span + 1 < spans)
+    crossed = jnp.logical_and(whole_spans, span > 0)
+    up_first, up_last = select([(jnp.logical_and(whole_spans, place == 3), side), (jnp.logical_and(crossing, place == 7), cross_up(span))])
+    dn_first, dn_last = select([(jnp.logical_and(whole_spans, place == 4), side), (jnp.logical_and(crossed, place == 0), cross_down(span))])
+    up_via = jnp.clip(jnp.where(place == 3, me + 4, me - 2), 0, n - 1)
+    dn_via = jnp.clip(jnp.where(place == 4, me - 4, me + 3), 0, n - 1)
+    relays_up = jnp.logical_and(whole_spans, jnp.logical_or(place == 7, jnp.logical_and(place == 5, crossing)))
+    relays_down = jnp.logical_and(whole_spans, jnp.logical_or(place == 0, jnp.logical_and(place == 3, crossed)))
+    near = jnp.logical_or(place == 7, place == 0)
+    rl_first, rl_last = select([
+        (jnp.logical_and(whole_spans, near), side),
+        (jnp.logical_and(crossing, place == 5), cross_up(span)),
+        (jnp.logical_and(crossed, place == 3), cross_down(span)),
+    ])
+    rl_target = jnp.clip(
+        jnp.where(place == 7, me - 3, jnp.where(place == 5, me + 3, jnp.where(place == 0, me + 3, me - 4))), 0, n - 1)
 
     def at(device):
         return dict(device_id=(device,), device_id_type=pl.DeviceIdType.MESH)
@@ -256,12 +297,46 @@
             self.wait_recv = lambda i: copy(i * crow * per, crow * per, i).wait_recv()
             self.wait_send = lambda: copy(first, ny - first, 0).wait_send()
 
+            def aside(c, unit):
+                return pl.ds(pl.multiple_of(unit * grow + lax.rem(c, group) * crow, 8), crow)
+
+            def detour(c, unit, via):
+                rows = pl.ds(pl.multiple_of(c * crow + src_pad, 8), crow)
+                pltpu.make_async_remote_copy(
+                    src[0].at[src[1], rows], relay.at[0, aside(c, unit)], send, relay_recv.at[unit], **at(via)).start()
+
+            def forward(c, unit):
+                rows = pl.ds(pl.multiple_of(c * crow + dst_pad, 8), crow)
+                pltpu.make_async_remote_copy(
+                    relay.at[0, aside(c, unit)], dst[0].at[dst[1], rows], relay_send.at[unit], recv.at[c // per],
+                    **at(rl_target)).start()
+
+            self.detour, self.forward = detour, forward
+
     lw_down = Flow((lw, 0), (lw_next, 0), send.at[0], lw_recv, low, group, 0, 0, raw_rows)
     z_down = Flow((z, 2), (z, depth + 2), send.at[1], dn_recv, low, group)
     y_down = Flow((y, 1), (y, depth + 1), send.at[2], yd_recv, low, group)
     top_up = Flow((part_z, 0), (z, 1), send.at[3], top_recv, high, group, 0)
     next_up = Flow((z, top + 1), (z, 0), send.at[4], next_recv, high, 1)
 
+    def send_chunk(flow, second, c, first, last, via):
+        unit = c // group + (head if second else head - plane_units)
+        aside = jnp.logical_and(unit >= first, unit < last)
+        when(aside, lambda: flow.detour(c, jnp.maximum(unit, 0), via))
+        when(jnp.logical_not(aside), lambda: flow.start(c))
+
+    def forward_unit(cond, unit, second):
+        def run(flow):
+            pltpu.make_async_remote_copy(
+                relay.at[0, pl.ds(0, grow)], relay.at[0, pl.ds(0, grow)], relay_send.at[unit], relay_recv.at[unit],
+                **at(rl_target)).wait_recv()
+            for i in range(group):
+                flow.forward((unit + (-head if second else plane_units - head)) * group + i, unit)
+
+        inside = jnp.logical_and(cond, jnp.logical_and(unit >= rl_first, unit < rl_last))
+        when(jnp.logical_and(inside, relays_up), lambda: run(next_up if second else top_up))
+        when(jnp.logical_and(inside, relays_down), lambda: run(z_down if second else lw_down))
+
     def flat(p, r):
         a = u[p, pl.ds(r, ROWS), :]
         b = v[p, pl.ds(r, ROWS + PAD), :]
@@ -277,8 +352,8 @@
         part_z[0, rows, :] = inv[top + 1, rows, :] * (flat(top, r) - lifted(top, r))
 
     def first_sends(c):
-        when(jnp.logical_and(has_low, c >= raw), lambda: lw_down.start(c))
-        when(has_high, lambda: top_up.start(c))
+        when(jnp.logical_and(has_low, c >= raw), lambda: send_chunk(lw_down, False, c, dn_first, dn_last, dn_via))
+        when(has_high, lambda: send_chunk(top_up, False, c, up_first, up_last, up_via))
 
     staged(lambda c: over(c, first_rows), first_sends)
 
@@ -290,9 +365,9 @@
     for p in range(top):
         def z_sends(c, p=p):
             if p == 0:
-                when(has_low, lambda: z_down.start(c))
+                when(has_low, lambda: send_chunk(z_down, True, c, dn_first, dn_last, dn_via))
             if p == top - 1:
-                when(has_high, lambda: next_up.start(c))
+                when(has_high, lambda: send_chunk(next_up, True, c, up_first, up_last, up_via))
         staged(lambda c, p=p: over(c, functools.partial(z_rows, p)), z_sends)
 
     @pl.when(has_high)
@@ -347,6 +422,8 @@
         when(jnp.logical_and(has_high, c >= raw // group), lambda: lw_down.wait_recv(c))
         when(has_low, lambda: top_up.wait_recv(c))
         over(c, low_rows, grow)
+        forward_unit(jnp.logical_and(near, c >= groups - few), every - groups + c, True)
+        forward_unit(jnp.logical_and(jnp.logical_not(near), lax.rem(c, 2) == 1), c // 2, False)
 
     def start_y(c):
         for i in range(group):
@@ -376,23 +453,25 @@
             when(has_low, lambda: next_up.wait_recv(chunk))
             when(jnp.logical_and(gating, chunk == chunks - LEAD), lambda: pl.semaphore_signal(
                 gate, inc=1, **at(jnp.minimum(me + SPAN - 2, n - 1))))
+        @pl.when(jnp.logical_and(gated, c == OPEN))
+        def _():
+            pl.semaphore_wait(gate, 1)
+
+            def start(i, carry):
+                start_y(i)
+                return carry
+
+            lax.fori_loop(0, groups, start, 0)
+
         over(c, high_rows, grow)
+        for i in range(2):
+            forward_unit(jnp.logical_and(jnp.logical_not(near), c < groups // 2), head + jnp.minimum(2 * c, groups - 2) + i, True)
 
     def image_rows(r):
         for p in range(depth):
             a_rows(p, r)
 
     staged(high_chunk, lambda c: over(c, image_rows, grow), groups)
-
-    @pl.when(gated)
-    def _():
-        pl.semaphore_wait(gate, 1)
-
-        def start(c, carry):
-            start_y(c)
-            return carry
-
-        lax.fori_loop(0, groups, start, 0)
 
     for j in range(6):
         t = jnp.sum(acc[j], axis=0, keepdims=True)
@@ -489,6 +568,13 @@
             flow.wait_send()
 
     mx_whole.wait_send()
+
+    def forwarded(unit, carry):
+        part = relay.at[0, pl.ds(0, grow)]
+        pltpu.make_async_remote_copy(part, part, relay_send.at[unit], relay_recv.at[unit], **at(rl_target)).wait_send()
+        return carry
+
+    lax.fori_loop(rl_first, rl_last, forwarded, 0)
 
 
 def store(w, s, w_hbm, s_hbm, sem):
@@ -532,6 +618,7 @@
                 pltpu.VMEM((1, ny, nx), f32),
                 pltpu.VMEM((1, ny, nx), f32),
                 pltpu.VMEM((1, raw * crow, nx), f32),
+                pltpu.VMEM((1, 3 * ny // 2, nx), f32),
                 pltpu.VMEM((depth + 3, nw, nx), i32),
                 pltpu.VMEM((depth + 1, 4, nw, nx), i32),
                 pltpu.VMEM((6, 8, nx), f32),
@@ -548,6 +635,7 @@
                 dma((5,)),
                 dma((chunks // group,)), dma((chunks // group,)), dma((chunks // group,)), dma((chunks // group,)),
                 dma((chunks,)),
+                dma((3 * chunks // group // 2,)), dma((3 * chunks // group // 2,)),
                 dma, dma, dma, dma,
                 dma((2,)), dma((2,)),
                 pltpu.SemaphoreType.REGULAR,

time: 131 us -> 126 us (0.962)
  Pallas kernels: 130 us -> 125 us
    pallas_call x1, Pallas kernels: 127 us -> 121 us  [local(): pl.pallas_call(functools.partial(kernel, n, chunks, group, raw), out_shap...]
where the time goes in v4:
time: 126 us; the launch traced here: 125 us
  Pallas kernels  125 us (99%)
    pallas_call x1, Pallas kernels, local(): pl.pallas_call(functools.partial(kernel, n, chunks, group, raw), out_shap...  121 us
    pallas_call x1, Pallas kernels, local(): pl.pallas_call(store, out_shape=(out, out), in_specs=[vmem_spec] * 2, out...  3.37 us

profile of v4, /device:TPU:1, one launch (start us, length us, event | category | flops | bytes accessed | tf_op | source)
XLA Modules:
  0.0 125.4 jit_solution(2078869077350984052)
XLA Ops:
  0.6 121.4 %smoke_step.1 = (f32[2,1024,512]{2,1,0:T(8,128)S(1)}, f32[2,1024,512]{2,1,0:T(8,128)S(1)}) custom-call(f32[2,1024,512]{2,1,0:T(8,128)} %u_hbm.1, f32[2,1024,512]{2,1,0:T(8,128)} %v_hbm.1, f32[2,1024,512]{2,1,0:T(8,128)} %w_hbm.1, f32[2,1024,512]{2,1,0:T(8,128)} %s_hbm.1, s32[2,32,512]{2,1,0:T(8,128)} %ob_hbm.1), custom_call_target="tpu_custom_call" | custom-call | tf_op jit(solution)/shard_map/smoke_step/pallas_call | solution.py:604
  122.1 3.4 %store.1 = (f32[2,1024,512]{2,1,0:T(8,128)}, f32[2,1024,512]{2,1,0:T(8,128)}) custom-call(f32[2,1024,512]{2,1,0:T(8,128)S(1)} %get-tuple-element.4.w, f32[2,1024,512]{2,1,0:T(8,128)S(1)} %get-tuple-element.5.s), custom_call_target="tpu_custom_call" | custom-call | tf_op jit(solution)/shard_map/store/pallas_call | solution.py:648

commit v5 on v4

--- a/solution.py
+++ b/solution.py
@@ -15,10 +15,11 @@
 PAD = 8
 SPAN = 8
 LEAD = 4
+LAG = 400
 OPEN = 5
 
 
-def kernel(n, chunks, group, raw, u_hbm, v_hbm, w_hbm, s_hbm, ob_hbm, w, s,
+def kernel(n, chunks, group, raw_rows, u_hbm, v_hbm, w_hbm, s_hbm, ob_hbm, w, s,
            u, v, z, part_z, y, code, inv, ay, lw, lw_next, s_next, relay, ob, cw, acc, cf, mx, mx_all, st, st_pair, st_all, total,
            in_sem, ob_send, ob_recv, raw_send, raw_recv, send, lw_recv, dn_recv, yd_recv, top_recv, next_recv, relay_recv, relay_send,
            mx_send, mx_recv, st_send, st_recv, pair_send, pair_recv, gate):
@@ -88,17 +89,16 @@
         part = pl.ds(first, rows)
         return pltpu.make_async_copy(src.at[p, part], dst.at[p, part], in_sem.at[k * depth + p if sem is None else sem])
 
-    raw_rows = raw * crow
     ob_in = pltpu.make_async_copy(ob_hbm, ob.at[pl.ds(2, depth)], in_sem.at[4 * depth])
     raw_in = [load(k, 0, 0, raw_rows, 4 * depth + k - 1) for k in (2, 3)]
     rest_in = {(k, p): load(k, p, raw_rows, ny - raw_rows) if k >= 2 and p == 0 else load(k, p)
                for k in range(4) for p in range(depth)}
+    scan = [(k, p) for k in range(3) for p in range(depth - 1, -1, -1)]
     ob_in.start()
+    for pair in scan:
+        rest_in[pair].start()
     for copy in raw_in:
         copy.start()
-    for (k, _), copy in rest_in.items():
-        if k < 3:
-            copy.start()
 
     barrier = pltpu.get_barrier_semaphore()
 
@@ -127,8 +127,6 @@
         lax.fori_loop(0, nb, body, 0)
 
     ob_in.wait()
-    for copy in raw_in:
-        copy.wait()
     pl.semaphore_wait(barrier, n - 1)
 
     ob_down = pltpu.make_async_remote_copy(
@@ -162,19 +160,20 @@
         zero_planes(z, (depth + 2,), PAD)
         zero_planes(lw_next, (0,), 0)
 
+    def largest(k, p, first, last, m):
+        def body(i, m):
+            a = jnp.abs(ins[k][1][p, pl.ds(pl.multiple_of(i * ROWS, 8), ROWS), :])
+            return jnp.maximum(m, jnp.max(a.reshape(ROWS // 8, 8, nx), axis=0))
+        return lax.fori_loop(first, last, body, m)
+
     peak = jnp.zeros((8, nx), jnp.float32)
-    for k in range(3):
-        ref = ins[k][1]
-        for p in range(depth):
-            rest_in[k, p].wait()
-            if k == 1:
-                rest_in[3, p].start()
-
-            def body(i, m, ref=ref, p=p):
-                a = jnp.abs(ref[p, pl.ds(pl.multiple_of(i * ROWS, 8), ROWS), :])
-                return jnp.maximum(m, jnp.max(a.reshape(ROWS // 8, 8, nx), axis=0))
-
-            peak = lax.fori_loop(0, nb, body, peak)
+    for k, p in scan:
+        rest_in[k, p].wait()
+        if k == 1:
+            rest_in[3, p].start()
+        peak = largest(k, p, raw_rows // ROWS if (k, p) == (2, 0) else 0, nb, peak)
+    raw_in[0].wait()
+    peak = largest(2, 0, 0, raw_rows // ROWS, peak)
     m = jnp.max(peak, axis=0, keepdims=True)
     part = m[:, 0:128]
     for c in range(128, nx, 128):
@@ -193,6 +192,7 @@
 
     mx_start, mx_whole = spread(mx, mx_all, mx_send, mx_recv, 1, n)
     mx_start()
+    raw_in[1].wait()
 
     @pl.when(has_low)
     def _():
@@ -251,6 +251,12 @@
 
     for p in range(depth):
         rest_in[3, p].wait()
+
+    def ready(b, carry):
+        code_rows(b)
+        return carry
+
+    lax.fori_loop(0, nb // 4, ready, 0)
     mx_whole.wait_recv()
     mx_all[0] = mx[...]
     fastest = jnp.max(jnp.max(mx_all[...], axis=0), axis=1, keepdims=True)
@@ -295,6 +301,8 @@
 
             self.start = lambda c: copy(c * crow, crow, c // per).start()
             self.wait_recv = lambda i: copy(i * crow * per, crow * per, i).wait_recv()
+            self.start_rest = lambda: copy(first, crow - first % crow, first // crow // per).start()
+            self.wait_rest = lambda: copy(first, grow - first, 0).wait_recv()
             self.wait_send = lambda: copy(first, ny - first, 0).wait_send()
 
             def aside(c, unit):
@@ -303,12 +311,12 @@
             def detour(c, unit, via):
                 rows = pl.ds(pl.multiple_of(c * crow + src_pad, 8), crow)
                 pltpu.make_async_remote_copy(
-                    src[0].at[src[1], rows], relay.at[0, aside(c, unit)], send, relay_recv.at[unit], **at(via)).start()
+                    src[0].at[src[1], rows], relay.at[0, aside(c, unit)], send, relay_recv.at[unit // 2], **at(via)).start()
 
             def forward(c, unit):
                 rows = pl.ds(pl.multiple_of(c * crow + dst_pad, 8), crow)
                 pltpu.make_async_remote_copy(
-                    relay.at[0, aside(c, unit)], dst[0].at[dst[1], rows], relay_send.at[unit], recv.at[c // per],
+                    relay.at[0, aside(c, unit)], dst[0].at[dst[1], rows], relay_send, recv.at[c // per],
                     **at(rl_target)).start()
 
             self.detour, self.forward = detour, forward
@@ -325,13 +333,15 @@
         when(aside, lambda: flow.detour(c, jnp.maximum(unit, 0), via))
         when(jnp.logical_not(aside), lambda: flow.start(c))
 
-    def forward_unit(cond, unit, second):
+    def set_aside(first, count):
+        part = relay.at[0, pl.ds(0, count * grow)]
+        return pltpu.make_async_remote_copy(part, part, relay_send, relay_recv.at[first // 2], **at(rl_target))
+
+    def forward_pair(cond, unit, second):
         def run(flow):
-            pltpu.make_async_remote_copy(
-                relay.at[0, pl.ds(0, grow)], relay.at[0, pl.ds(0, grow)], relay_send.at[unit], relay_recv.at[unit],
-                **at(rl_target)).wait_recv()
-            for i in range(group):
-                flow.forward((unit + (-head if second else plane_units - head)) * group + i, unit)
+            set_aside(unit, 2).wait_recv()
+            for i in range(2 * group):
+                flow.forward((unit + (-head if second else plane_units - head)) * group + i, unit + i // group)
 
         inside = jnp.logical_and(cond, jnp.logical_and(unit >= rl_first, unit < rl_last))
         when(jnp.logical_and(inside, relays_up), lambda: run(next_up if second else top_up))
@@ -345,17 +355,27 @@
     def inner_rows(r):
         return pl.ds(pl.multiple_of(r + PAD, 8), ROWS)
 
+    def lw_rows(r):
+        lw[0, pl.ds(r, ROWS), :] = lifted(0, r)
+
+    def shifted(c):
+        return lax.rem(c + raw_rows // crow, chunks)
+
+    def lw_sends(c):
+        when(jnp.logical_and(has_low, c * crow >= raw_rows),
+             lambda: send_chunk(lw_down, False, c, dn_first, dn_last, dn_via))
+        if raw_rows % crow:
+            when(jnp.logical_and(has_low, c == raw_rows // crow), lw_down.start_rest)
+
+    staged(lambda c: over(shifted(c), lw_rows), lambda c: lw_sends(shifted(c)))
+
     def first_rows(r):
-        code_rows(r // ROWS)
+        when(r >= ny // 4, lambda: code_rows(r // ROWS))
         rows = pl.ds(r, ROWS)
-        lw[0, rows, :] = lifted(0, r)
         part_z[0, rows, :] = inv[top + 1, rows, :] * (flat(top, r) - lifted(top, r))
 
-    def first_sends(c):
-        when(jnp.logical_and(has_low, c >= raw), lambda: send_chunk(lw_down, False, c, dn_first, dn_last, dn_via))
-        when(has_high, lambda: send_chunk(top_up, False, c, up_first, up_last, up_via))
-
-    staged(lambda c: over(c, first_rows), first_sends)
+    staged(lambda c: over(c, first_rows),
+           lambda c: when(has_high, lambda: send_chunk(top_up, False, c, up_first, up_last, up_via)))
 
     def z_rows(p, r):
         rows = pl.ds(r, ROWS)
@@ -419,11 +439,13 @@
             y_rows(p, r)
 
     def low_chunk(c):
-        when(jnp.logical_and(has_high, c >= raw // group), lambda: lw_down.wait_recv(c))
+        when(jnp.logical_and(has_high, c > 0), lambda: lw_down.wait_recv(c))
+        if raw_rows < grow:
+            when(jnp.logical_and(has_high, c == 0), lw_down.wait_rest)
         when(has_low, lambda: top_up.wait_recv(c))
         over(c, low_rows, grow)
-        forward_unit(jnp.logical_and(near, c >= groups - few), every - groups + c, True)
-        forward_unit(jnp.logical_and(jnp.logical_not(near), lax.rem(c, 2) == 1), c // 2, False)
+        forward_pair(jnp.logical_and(near, c == groups - 1), every - few, True)
+        forward_pair(jnp.logical_and(jnp.logical_not(near), lax.rem(c, 4) == 3), c // 4 * 2, False)
 
     def start_y(c):
         for i in range(group):
@@ -451,8 +473,12 @@
         for i in range(group):
             chunk = c * group + i
             when(has_low, lambda: next_up.wait_recv(chunk))
-            when(jnp.logical_and(gating, chunk == chunks - LEAD), lambda: pl.semaphore_signal(
-                gate, inc=1, **at(jnp.minimum(me + SPAN - 2, n - 1))))
+
+            @pl.when(jnp.logical_and(gating, chunk == chunks - LEAD))
+            def _():
+                pl.delay(LAG)
+                pl.semaphore_signal(gate, inc=1, **at(jnp.minimum(me + SPAN - 2, n - 1)))
+
         @pl.when(jnp.logical_and(gated, c == OPEN))
         def _():
             pl.semaphore_wait(gate, 1)
@@ -464,8 +490,7 @@
             lax.fori_loop(0, groups, start, 0)
 
         over(c, high_rows, grow)
-        for i in range(2):
-            forward_unit(jnp.logical_and(jnp.logical_not(near), c < groups // 2), head + jnp.minimum(2 * c, groups - 2) + i, True)
+        forward_pair(jnp.logical_and(jnp.logical_not(near), c < groups // 2), head + jnp.minimum(2 * c, groups - 2), True)
 
     def image_rows(r):
         for p in range(depth):
@@ -569,12 +594,8 @@
 
     mx_whole.wait_send()
 
-    def forwarded(unit, carry):
-        part = relay.at[0, pl.ds(0, grow)]
-        pltpu.make_async_remote_copy(part, part, relay_send.at[unit], relay_recv.at[unit], **at(rl_target)).wait_send()
-        return carry
-
-    lax.fori_loop(rl_first, rl_last, forwarded, 0)
+    for count in (few, head, 2 * head, every):
+        when(rl_last - rl_first == count, lambda count=count: set_aside(0, count).wait_send())
 
 
 def store(w, s, w_hbm, s_hbm, sem):
@@ -594,15 +615,15 @@
     def local(u_face, v_face, w_face, smoke, obstacles):
         depth, ny, nx = u_face.shape
         nw = obstacles.shape[1]
-        chunks, group, raw = 16, 2, 2
-        crow = ny // chunks
+        chunks, group = 16, 2
+        raw_rows = 3 * ny // 32
         f32, i32 = jnp.float32, jnp.int32
         dma = pltpu.SemaphoreType.DMA
         any_spec = pl.BlockSpec(memory_space=pl.ANY)
         vmem_spec = pl.BlockSpec(memory_space=pltpu.VMEM)
         shape = pltpu.VMEM((depth, ny, nx), f32)
         results = pl.pallas_call(
-            functools.partial(kernel, n, chunks, group, raw),
+            functools.partial(kernel, n, chunks, group, raw_rows),
             out_shape=(shape, shape),
             in_specs=[any_spec] * 5,
             out_specs=(vmem_spec, vmem_spec),
@@ -617,7 +638,7 @@
                 pltpu.VMEM((depth, ny, nx), f32),
                 pltpu.VMEM((1, ny, nx), f32),
                 pltpu.VMEM((1, ny, nx), f32),
-                pltpu.VMEM((1, raw * crow, nx), f32),
+                pltpu.VMEM((1, raw_rows, nx), f32),
                 pltpu.VMEM((1, 3 * ny // 2, nx), f32),
                 pltpu.VMEM((depth + 3, nw, nx), i32),
                 pltpu.VMEM((depth + 1, 4, nw, nx), i32),
@@ -635,7 +656,7 @@
                 dma((5,)),
                 dma((chunks // group,)), dma((chunks // group,)), dma((chunks // group,)), dma((chunks // group,)),
                 dma((chunks,)),
-                dma((3 * chunks // group // 2,)), dma((3 * chunks // group // 2,)),
+                dma((3 * chunks // group // 4,)), dma,
                 dma, dma, dma, dma,
                 dma((2,)), dma((2,)),
                 pltpu.SemaphoreType.REGULAR,

time: 126 us -> 125 us (level)
  no operation moved by 1% of the time
where the time goes in v5:
time: 125 us
  Pallas kernels  124 us (99%)
    pallas_call x1, Pallas kernels, local(): pl.pallas_call(functools.partial(kernel, n, chunks, group, raw_rows), out...  121 us
    pallas_call x1, Pallas kernels, local(): pl.pallas_call(store, out_shape=(out, out), in_specs=[vmem_spec] * 2, out...  3.37 us

profile of v5, /device:TPU:1, one launch (start us, length us, event | category | flops | bytes accessed | tf_op | source)
XLA Modules:
  0.0 125.0 jit_solution(6725023396167571635)
XLA Ops:
  0.6 121.0 %smoke_step.1 = (f32[2,1024,512]{2,1,0:T(8,128)S(1)}, f32[2,1024,512]{2,1,0:T(8,128)S(1)}) custom-call(f32[2,1024,512]{2,1,0:T(8,128)} %u_hbm.1, f32[2,1024,512]{2,1,0:T(8,128)} %v_hbm.1, f32[2,1024,512]{2,1,0:T(8,128)} %w_hbm.1, f32[2,1024,512]{2,1,0:T(8,128)} %s_hbm.1, s32[2,32,512]{2,1,0:T(8,128)} %ob_hbm.1), custom_call_target="tpu_custom_call" | custom-call | tf_op jit(solution)/shard_map/smoke_step/pallas_call | solution.py:625
  121.6 3.4 %store.1 = (f32[2,1024,512]{2,1,0:T(8,128)}, f32[2,1024,512]{2,1,0:T(8,128)}) custom-call(f32[2,1024,512]{2,1,0:T(8,128)S(1)} %get-tuple-element.4.w, f32[2,1024,512]{2,1,0:T(8,128)S(1)} %get-tuple-element.5.s), custom_call_target="tpu_custom_call" | custom-call | tf_op jit(solution)/shard_map/store/pallas_call | solution.py:669

commit v6 on v5

--- a/solution.py
+++ b/solution.py
@@ -15,7 +15,7 @@
 PAD = 8
 SPAN = 8
 LEAD = 4
-LAG = 400
+LAG = 700
 OPEN = 5
 
 
@@ -498,13 +498,12 @@
 
     staged(high_chunk, lambda c: over(c, image_rows, grow), groups)
 
+    lanes = lax.broadcasted_iota(jnp.int32, (1, 128), 1)
+    sums = jnp.zeros((1, 128), jnp.float32)
     for j in range(6):
-        t = jnp.sum(acc[j], axis=0, keepdims=True)
-        part = t[:, 0:128]
-        for c in range(128, nx, 128):
-            part = part + t[:, c : c + 128]
-        st[j : j + 1, :] = part
-    st[6:8, :] = jnp.zeros((2, 128), jnp.float32)
+        t = jnp.sum(jnp.sum(acc[j], axis=0, keepdims=True), axis=1, keepdims=True)
+        sums = jnp.where(lanes == j, jnp.broadcast_to(t, (1, 128)), sums)
+    st[...] = sums
 
     pair_in = pltpu.make_async_remote_copy(st, st_pair, pair_send.at[0], pair_recv.at[0], **at(partner))
     pair_out = pltpu.make_async_remote_copy(total, total, pair_send.at[1], pair_recv.at[1], **at(partner))
@@ -534,9 +533,11 @@
         pair_in.wait_send()
         pair_out.wait_recv()
 
-    sums = jnp.broadcast_to(jnp.sum(total[...], axis=1, keepdims=True), (8, nx))
-    gamma, squares, fluid = sums[0:1], sums[1:2], sums[2:3]
-    delta, eta, theta = sums[3:4], sums[4:5], sums[5:6]
+    def summed(j):
+        t = jnp.sum(jnp.where(lanes == j, total[...], 0.0), axis=1, keepdims=True)
+        return jnp.broadcast_to(t, (1, nx))
+
+    gamma, squares, fluid, delta, eta, theta = (summed(j) for j in range(6))
     alpha = gamma / delta
     gamma_next = gamma - 2.0 * alpha * delta + alpha * alpha * eta
     beta = gamma_next / gamma
@@ -646,10 +647,10 @@
                 pltpu.VMEM((8, nx), f32),
                 pltpu.VMEM((1, 128), f32),
                 pltpu.VMEM((n, 1, 128), f32),
-                pltpu.VMEM((8, 128), f32),
-                pltpu.VMEM((8, 128), f32),
-                pltpu.VMEM((n // 2, 8, 128), f32),
-                pltpu.VMEM((8, 128), f32),
+                pltpu.VMEM((1, 128), f32),
+                pltpu.VMEM((1, 128), f32),
+                pltpu.VMEM((n // 2, 1, 128), f32),
+                pltpu.VMEM((1, 128), f32),
                 dma((4 * depth + 3,)),
                 dma((2,)), dma((2,)),
                 dma((2,)), dma((2,)),

time: 125 us -> 125 us (level)
  no operation moved by 1% of the time
where the time goes in v6:
time: 125 us
  Pallas kernels  124 us (99%)
    pallas_call x1, Pallas kernels, local(): pl.pallas_call(functools.partial(kernel, n, chunks, group, raw_rows), out...  121 us
    pallas_call x1, Pallas kernels, local(): pl.pallas_call(store, out_shape=(out, out), in_specs=[vmem_spec] * 2, out...  3.37 us

profile of v6, /device:TPU:1, one launch (start us, length us, event | category | flops | bytes accessed | tf_op | source)
XLA Modules:
  0.0 124.7 jit_solution(17055784026312364833)
XLA Ops:
  0.6 120.7 %smoke_step.1 = (f32[2,1024,512]{2,1,0:T(8,128)S(1)}, f32[2,1024,512]{2,1,0:T(8,128)S(1)}) custom-call(f32[2,1024,512]{2,1,0:T(8,128)} %u_hbm.1, f32[2,1024,512]{2,1,0:T(8,128)} %v_hbm.1, f32[2,1024,512]{2,1,0:T(8,128)} %w_hbm.1, f32[2,1024,512]{2,1,0:T(8,128)} %s_hbm.1, s32[2,32,512]{2,1,0:T(8,128)} %ob_hbm.1), custom_call_target="tpu_custom_call" | custom-call | tf_op jit(solution)/shard_map/smoke_step/pallas_call | solution.py:626
  121.3 3.4 %store.1 = (f32[2,1024,512]{2,1,0:T(8,128)}, f32[2,1024,512]{2,1,0:T(8,128)}) custom-call(f32[2,1024,512]{2,1,0:T(8,128)S(1)} %get-tuple-element.4.w, f32[2,1024,512]{2,1,0:T(8,128)S(1)} %get-tuple-element.5.s), custom_call_target="tpu_custom_call" | custom-call | tf_op jit(solution)/shard_map/store/pallas_call | solution.py:670

commit v7 on v6

--- a/solution.py
+++ b/solution.py
@@ -137,9 +137,11 @@
     raw_part = pl.ds(0, raw_rows)
     raw_copies = [
         pltpu.make_async_remote_copy(
-            src.at[0, raw_part], dst.at[0, raw_part], raw_send.at[j], raw_recv.at[j], **at(low))
-        for j, (src, dst) in enumerate([(w, lw_next), (s, s_next)])
+            src.at[0, raw_part], dst.at[0, raw_part], raw_send, raw_recv, **at(low))
+        for src, dst in [(w, lw_next), (s, s_next)]
     ]
+    both = lw_next.at[0, pl.ds(0, 2 * raw_rows)]
+    raw_whole = pltpu.make_async_remote_copy(both, both, raw_send, raw_recv, **at(low))
 
     @pl.when(has_low)
     def _():
@@ -303,7 +305,6 @@
             self.wait_recv = lambda i: copy(i * crow * per, crow * per, i).wait_recv()
             self.start_rest = lambda: copy(first, crow - first % crow, first // crow // per).start()
             self.wait_rest = lambda: copy(first, grow - first, 0).wait_recv()
-            self.wait_send = lambda: copy(first, ny - first, 0).wait_send()
 
             def aside(c, unit):
                 return pl.ds(pl.multiple_of(unit * grow + lax.rem(c, group) * crow, 8), crow)
@@ -322,10 +323,10 @@
             self.detour, self.forward = detour, forward
 
     lw_down = Flow((lw, 0), (lw_next, 0), send.at[0], lw_recv, low, group, 0, 0, raw_rows)
-    z_down = Flow((z, 2), (z, depth + 2), send.at[1], dn_recv, low, group)
-    y_down = Flow((y, 1), (y, depth + 1), send.at[2], yd_recv, low, group)
-    top_up = Flow((part_z, 0), (z, 1), send.at[3], top_recv, high, group, 0)
-    next_up = Flow((z, top + 1), (z, 0), send.at[4], next_recv, high, 1)
+    z_down = Flow((z, 2), (z, depth + 2), send.at[0], dn_recv, low, group)
+    y_down = Flow((y, 1), (y, depth + 1), send.at[0], yd_recv, low, 2 * group)
+    top_up = Flow((part_z, 0), (z, 1), send.at[1], top_recv, high, group, 0)
+    next_up = Flow((z, top + 1), (z, 0), send.at[1], next_recv, high, 1)
 
     def send_chunk(flow, second, c, first, last, via):
         unit = c // group + (head if second else head - plane_units)
@@ -392,8 +393,7 @@
 
     @pl.when(has_high)
     def _():
-        for copy in raw_copies:
-            copy.wait_recv()
+        raw_whole.wait_recv()
 
         def lift(i, carry):
             rows = pl.ds(pl.multiple_of(i * ROWS, 8), ROWS)
@@ -505,8 +505,8 @@
         sums = jnp.where(lanes == j, jnp.broadcast_to(t, (1, 128)), sums)
     st[...] = sums
 
-    pair_in = pltpu.make_async_remote_copy(st, st_pair, pair_send.at[0], pair_recv.at[0], **at(partner))
-    pair_out = pltpu.make_async_remote_copy(total, total, pair_send.at[1], pair_recv.at[1], **at(partner))
+    pair_in = pltpu.make_async_remote_copy(st, st_pair, pair_send, pair_recv, **at(partner))
+    pair_out = pltpu.make_async_remote_copy(total, total, pair_send, pair_recv, **at(partner))
     st_start, st_whole = spread(st_pair, st_all, st_send, st_recv, 2, n // 2)
 
     @pl.when(even)
@@ -525,8 +525,7 @@
 
     @pl.when(has_low)
     def _():
-        for copy in raw_copies:
-            copy.wait_send()
+        raw_whole.wait_send()
 
     @pl.when(even)
     def _():
@@ -573,7 +572,7 @@
     @pl.when(has_high)
     def _():
         def last_chunk(c, carry):
-            y_down.wait_recv(c)
+            when(lax.rem(c, 2) == 0, lambda: y_down.wait_recv(c // 2))
             over(c, last_rows, grow)
             return carry
         lax.fori_loop(0, groups, last_chunk, 0)
@@ -583,15 +582,12 @@
         st_whole.wait_send()
         pair_out.wait_send()
 
-    @pl.when(has_low)
-    def _():
-        for flow in (lw_down, z_down, y_down):
-            flow.wait_send()
-
-    @pl.when(has_high)
-    def _():
-        for flow in (top_up, next_up):
-            flow.wait_send()
+    def all_sent(index, planes, rows):
+        part = code.at[pl.ds(0, planes), pl.ds(0, rows)]
+        pltpu.make_async_remote_copy(part, part, send.at[index], lw_recv.at[0], **at(low)).wait_send()
+
+    when(has_low, lambda: all_sent(0, 3, ny - raw_rows // 3))
+    when(has_high, lambda: all_sent(1, 2, ny))
 
     mx_whole.wait_send()
 
@@ -653,13 +649,13 @@
                 pltpu.VMEM((1, 128), f32),
                 dma((4 * depth + 3,)),
                 dma((2,)), dma((2,)),
-                dma((2,)), dma((2,)),
-                dma((5,)),
-                dma((chunks // group,)), dma((chunks // group,)), dma((chunks // group,)), dma((chunks // group,)),
+                dma, dma,
+                dma((2,)),
+                dma((chunks // group,)), dma((chunks // group,)), dma((chunks // group // 2,)), dma((chunks // group,)),
                 dma((chunks,)),
                 dma((3 * chunks // group // 4,)), dma,
                 dma, dma, dma, dma,
-                dma((2,)), dma((2,)),
+                dma, dma,
                 pltpu.SemaphoreType.REGULAR,
             ],
             compiler_params=pltpu.CompilerParams(

time: 125 us -> 125 us (level)
  no operation moved by 1% of the time
where the time goes in v7:
time: 125 us
  Pallas kernels  124 us (99%)
    pallas_call x1, Pallas kernels, local(): pl.pallas_call(functools.partial(kernel, n, chunks, group, raw_rows), out...  121 us
    pallas_call x1, Pallas kernels, local(): pl.pallas_call(store, out_shape=(out, out), in_specs=[vmem_spec] * 2, out...  3.37 us

profile of v7, /device:TPU:1, one launch (start us, length us, event | category | flops | bytes accessed | tf_op | source)
XLA Modules:
  0.0 124.6 jit_solution(7042161890778590142)
XLA Ops:
  0.6 120.6 %smoke_step.1 = (f32[2,1024,512]{2,1,0:T(8,128)S(1)}, f32[2,1024,512]{2,1,0:T(8,128)S(1)}) custom-call(f32[2,1024,512]{2,1,0:T(8,128)} %u_hbm.1, f32[2,1024,512]{2,1,0:T(8,128)} %v_hbm.1, f32[2,1024,512]{2,1,0:T(8,128)} %w_hbm.1, f32[2,1024,512]{2,1,0:T(8,128)} %s_hbm.1, s32[2,32,512]{2,1,0:T(8,128)} %ob_hbm.1), custom_call_target="tpu_custom_call" | custom-call | tf_op jit(solution)/shard_map/smoke_step/pallas_call | solution.py:622
  121.3 3.4 %store.1 = (f32[2,1024,512]{2,1,0:T(8,128)}, f32[2,1024,512]{2,1,0:T(8,128)}) custom-call(f32[2,1024,512]{2,1,0:T(8,128)S(1)} %get-tuple-element.4.w, f32[2,1024,512]{2,1,0:T(8,128)S(1)} %get-tuple-element.5.s), custom_call_target="tpu_custom_call" | custom-call | tf_op jit(solution)/shard_map/store/pallas_call | solution.py:666

commit v8 on v7

--- a/solution.py
+++ b/solution.py
@@ -16,7 +16,7 @@
 SPAN = 8
 LEAD = 4
 LAG = 700
-OPEN = 5
+OPEN = 6
 
 
 def kernel(n, chunks, group, raw_rows, u_hbm, v_hbm, w_hbm, s_hbm, ob_hbm, w, s,

time: 125 us -> 125 us (level)
  no operation moved by 1% of the time
where the time goes in v8:
time: 125 us
  Pallas kernels  124 us (99%)
    pallas_call x1, Pallas kernels, local(): pl.pallas_call(functools.partial(kernel, n, chunks, group, raw_rows), out...  121 us
    pallas_call x1, Pallas kernels, local(): pl.pallas_call(store, out_shape=(out, out), in_specs=[vmem_spec] * 2, out...  3.37 us

profile of v8, /device:TPU:1, one launch (start us, length us, event | category | flops | bytes accessed | tf_op | source)
XLA Modules:
  0.0 124.6 jit_solution(4207033660360091637)
XLA Ops:
  0.6 120.6 %smoke_step.1 = (f32[2,1024,512]{2,1,0:T(8,128)S(1)}, f32[2,1024,512]{2,1,0:T(8,128)S(1)}) custom-call(f32[2,1024,512]{2,1,0:T(8,128)} %u_hbm.1, f32[2,1024,512]{2,1,0:T(8,128)} %v_hbm.1, f32[2,1024,512]{2,1,0:T(8,128)} %w_hbm.1, f32[2,1024,512]{2,1,0:T(8,128)} %s_hbm.1, s32[2,32,512]{2,1,0:T(8,128)} %ob_hbm.1), custom_call_target="tpu_custom_call" | custom-call | tf_op jit(solution)/shard_map/smoke_step/pallas_call | solution.py:622
  121.3 3.4 %store.1 = (f32[2,1024,512]{2,1,0:T(8,128)}, f32[2,1024,512]{2,1,0:T(8,128)}) custom-call(f32[2,1024,512]{2,1,0:T(8,128)S(1)} %get-tuple-element.4.w, f32[2,1024,512]{2,1,0:T(8,128)S(1)} %get-tuple-element.5.s), custom_call_target="tpu_custom_call" | custom-call | tf_op jit(solution)/shard_map/store/pallas_call | solution.py:666
